TPU v7x, 32 devices: a whole 2x2x4 slice. The times are simulated.
32 devices in a mesh: gx: 2 (over core), gy: 2 (over x), gz: 8 (over z, y).
Axes of the slice: x: 2, y: 2, z: 4, core: 2. Of those that a mesh axis runs over, the one named last changes fastest.
Arguments:
- old_pos: float32 [3, 32768], P(None, ('gx', 'gy', 'gz')), may hold values from -6 to 6
- new_pos: float32 [3, 32768], P(None, ('gx', 'gy', 'gz')), may hold values from -6 to 6
- inv_mass: float32 [32768], P(('gx', 'gy', 'gz')), may hold values from 0.05 to 1
- rest_length: float32 [32768], P(('gx', 'gy', 'gz')), may hold values from 0.8 to 1.6
- bond_pairs: int32 [2, 32768], P(None, ('gx', 'gy', 'gz')), may hold values from 0 to 1311, as said below
- live: int32 [32768], P(('gx', 'gy', 'gz')), may hold values from 0 to 1, as said below
- send_index: int32 [192, 48], P(('gx', 'gy', 'gz')), may hold values from 0 to 1023, as said below
Outputs:
- displacement: float32 [3, 32768], P(None, ('gx', 'gy', 'gz'))
- multipliers: float32 [32768], P(('gx', 'gy', 'gz'))
Inputs may be any that keep to these rules, and one draw needn't show every extreme that they name: `bond_pairs`: in domain k's slots, row 0 is an own atom (0 to 1023). Row 1 indexes the domain's extended list: its own atoms, then six blocks of 48 received atoms, block 2a + s holding, in order, list 2a + s of the neighbour one step down (s = 0) or up (s = 1) along axis a. Every atom is in at most two live constraints, each received atom is the second atom of at most one live constraint, and exactly 216 live constraints of each domain name a received atom. `live`: padding slots change nothing. `send_index`: rows 6k to 6k + 5 are domain k's lists of own atoms; list 2a + s goes to the neighbour one step up (s = 0) or down (s = 1) along axis a, periodically. The 288 entries of a domain are distinct.
All inputs are finite; a program needn't handle non-finite values.
Results may differ from a plain program's by a relative error of at most 0.0001.
Values sent between devices are 32-bit elements; how exact they have to be, the bound alone decides.
No kernel may reach another device: no remote copies, remote signals or barrier semaphores. Data moves between devices by JAX's collectives and lax.ppermute only.
A program may use at most 64 MiB of HBM per device.

v0:
```python
import functools
import itertools

import jax
import jax.numpy as jnp
import numpy as np
from jax import lax
from jax.experimental import pallas as pl
from jax.experimental.pallas import tpu as pltpu
from jax.sharding import PartitionSpec as P

ORDER = 4
AXES = ("gx", "gy", "gz")
LANES = 128
HALF = LANES // 2
SUB = 8
CHUNK = 8
FIELDS = 12
REACH = 2 * (ORDER + 1)
VMEM = pl.BlockSpec(memory_space=pltpu.VMEM)
SMEM = pl.BlockSpec(memory_space=pltpu.SMEM)


def wide(row):
    return jnp.broadcast_to(row, (SUB, LANES))


def pick(tables, row, lane):
    total = jnp.zeros((SUB, LANES), jnp.float32)
    for number, load in tables.items():
        got = jnp.take_along_axis(wide(load()), lane, axis=1, mode="promise_in_bounds")
        total = jnp.where(row == number, got.astype(jnp.float32), total)
    return total


def flat_rows(ref, q):
    return {r: functools.partial(lambda q, r: ref[q : q + 1, r * LANES : (r + 1) * LANES], q, r) for r in range(SUB)}


def tile_rows(ref, base=0):
    return {r: functools.partial(lambda r: ref[base + r : base + r + 1, :], r) for r in range(SUB)}


def stack_rows(ref, q, hold):
    for r in range(SUB):
        hold[r : r + 1, :] = ref[q : q + 1, r * LANES : (r + 1) * LANES]
    return hold[...]


def sent_kernel(old, new, mass, send, out_x, out_y, out_z, where, pad):
    width = send.shape[1]
    pad[...] = jnp.zeros_like(pad)
    pad[0:6, 0:width] = send[...]
    low = pad[...]
    high = pltpu.roll(low, HALF, 1)
    where[...] = jnp.zeros_like(where)
    for a in range(3):
        where[a : a + 1, :] = low[2 * a : 2 * a + 1] + high[2 * a + 1 : 2 * a + 2]
    index = where[...]
    row, lane = index >> 7, index & (LANES - 1)
    tables = [flat_rows(old, q) for q in range(3)] + [flat_rows(new, q) for q in range(3)] + [tile_rows(mass)]
    outs = (out_x, out_y, out_z)
    for a in range(3):
        outs[a][...] = jnp.zeros_like(outs[a])
    for f, table in enumerate(tables):
        got = pick(table, row, lane)
        for a in range(3):
            outs[a][f : f + 1, :] = got[a : a + 1, :]


def second_place(second, width):
    atoms = SUB * LANES
    slot = second - atoms
    block = jnp.zeros_like(second)
    for b in range(1, 6):
        block = block + (slot >= b * width).astype(jnp.int32)
    lane = slot - block * width + (block & 1) * HALF
    remote = second >= atoms
    row = jnp.where(remote, 12 + (block >> 1), second >> 7)
    return row, jnp.where(remote, lane, second & (LANES - 1))


def nt_dot(a, b):
    return lax.dot_general(a, b, (((1,), (1,)), ((), ())), preferred_element_type=jnp.float32)


def split_codes(hit, code):
    code = jnp.broadcast_to(code, hit.shape)
    zero = jnp.zeros_like(code)
    both = jnp.concatenate([jnp.where(hit, code >> 4, zero), jnp.where(hit, code & 15, zero)], 0)
    return both.astype(jnp.float32).astype(jnp.bfloat16)


def lane_hits(lane, count):
    hits = lax.broadcasted_iota(jnp.int32, (LANES, count), 0) == jnp.broadcast_to(lane, (LANES, count))
    return jnp.where(hits, 1.0, 0.0).astype(jnp.bfloat16)


def link_kernel(width, bonds, live_row, live, where, links, hold_a, hold_b, s_ref):
    atoms = SUB * LANES
    first_row = bonds[0:1, :]
    second_row = bonds[1:2, :]
    usable = (live_row[...] != 0) & (first_row != second_row)
    node = lax.broadcasted_iota(jnp.int32, (1, atoms), 1)
    targets = lax.broadcasted_iota(jnp.int32, (2 * SUB, atoms), 0)
    total = jnp.zeros((4 * SUB, LANES), jnp.float32)
    places = ((first_row >> 7, first_row & (LANES - 1)), second_place(second_row, width))
    for end, (row, lane) in enumerate(places):
        row = jnp.where(usable, row, -1)
        hit = targets == jnp.broadcast_to(row, targets.shape)
        total = total + nt_dot(split_codes(hit, 2 * node + end + 1), lane_hits(lane, atoms))
    sums = 16.0 * total[: 2 * SUB] + total[2 * SUB :]

    index = where[...]
    lanes = lax.broadcasted_iota(jnp.int32, (1, LANES), 1)
    valid = ((lanes & (HALF - 1)) < width)
    small = lax.broadcasted_iota(jnp.int32, (SUB, LANES), 0)
    slots = jnp.zeros((2 * SUB, LANES), jnp.float32)
    for a in range(3):
        one = index[a : a + 1, :]
        row = jnp.where(valid, one >> 7, -1)
        hit = small == jnp.broadcast_to(row, small.shape)
        slots = slots + nt_dot(split_codes(hit, (SUB + a) * LANES + lanes + 1), lane_hits(one & (LANES - 1), LANES))
    sent_slot = 16.0 * slots[:SUB] + slots[SUB:]
    s_ref[0:SUB, :] = 4096.0 * sums[:SUB] + sent_slot
    out_code = sums[SUB:]

    first = stack_rows(bonds, 0, hold_a)
    second = stack_rows(bonds, 1, hold_b)
    alive = (live[...] != 0) & (first != second)
    me = lax.broadcasted_iota(jnp.int32, (SUB, LANES), 0) * LANES + lax.broadcasted_iota(jnp.int32, (SUB, LANES), 1)
    none = 2 * (2 * atoms - 1)
    table = tile_rows(s_ref)
    srow, slane = second_place(second, width)
    for end, (row, lane) in enumerate(((first >> 7, first & (LANES - 1)), (srow, slane))):
        both = pick(table, row, lane).astype(jnp.int32)
        code = (both >> 12) - (2 * me + end + 1)
        ghost = both & 4095
        link = jnp.where(code > 0, code - 1, jnp.where(ghost > 0, 2 * (ghost - 1), none))
        if end == 1:
            link = jnp.where(row >= SUB, 2 * (row * LANES + lane), link)
        links[end * SUB : (end + 1) * SUB, :] = jnp.where(alive, link, none).astype(jnp.float32)
    sent = pick(table, index >> 7, index & (LANES - 1)).astype(jnp.int32) >> 12
    sublane = lax.broadcasted_iota(jnp.int32, (SUB, LANES), 0)
    in_row = (sublane < 3) & ((lax.broadcasted_iota(jnp.int32, (SUB, LANES), 1) & (HALF - 1)) < width)
    ends = jnp.where(in_row, sent - 1, jnp.where(sublane >= 4, out_code.astype(jnp.int32) - 1, -1))
    links[2 * SUB : 3 * SUB, :] = ends.astype(jnp.float32)


def node_kernel(width, old, new, mass, rest, live, bonds, links, *refs):
    arrived = refs[:6]
    pub, hold_a, hold_b, got_ref = refs[6:]
    first = stack_rows(bonds, 0, hold_a)
    second = stack_rows(bonds, 1, hold_b)
    lower = lax.broadcasted_iota(jnp.int32, (1, LANES), 1) < HALF
    for a in range(3):
        got_ref[a * SUB : (a + 1) * SUB, :] = jnp.where(lower, arrived[2 * a][...], arrived[2 * a + 1][...])
    row, lane = first >> 7, first & (LANES - 1)
    srow, slane = second_place(second, width)
    tables = [flat_rows(old, q) for q in range(3)] + [flat_rows(new, q) for q in range(3)] + [tile_rows(mass)]
    firsts, seconds = [], []
    for f, table in enumerate(tables):
        firsts.append(pick(table, row, lane))
        more = dict(table)
        for a in range(3):
            more[12 + a] = functools.partial(lambda at: got_ref[at : at + 1, :], a * SUB + f)
        seconds.append(pick(more, srow, slane))
    span = [x - y for x, y in zip(firsts, seconds)]
    alive = live[...].astype(jnp.float32)
    scaling = alive * lax.rsqrt(firsts[6] + seconds[6])
    norm = lax.rsqrt(span[0] * span[0] + span[1] * span[1] + span[2] * span[2] + 0.25)
    values = [scaling * norm * span[q] for q in range(3)]
    values = values + [scaling * span[3 + q] for q in range(3)]
    values = values + [scaling * rest[...], firsts[6], seconds[6]]
    for f, value in enumerate(values):
        pub[f * SUB : (f + 1) * SUB, :] = value
    pub[9 * SUB : 12 * SUB, :] = links[...]


def place(dart):
    return dart >> 8, (dart >> 1) & (LANES - 1)


def main_kernel(
    counts, split, width, source, slot, near, bonds, mass, where, *refs
):
    shifts = len(split)
    pubs = refs[:shifts]
    (
        out_disp, out_mult, u_ref, n_ref, rho_ref, mf_ref, mg_ref, p_ref, e_ref,
        eu_ref, g_ref, w_ref, diag_ref, xa, xb, one_ref, two_ref, ep_ref, hold_a, hold_b,
    ) = refs[shifts:]

    start = 0
    for shift in range(shifts):
        pub = pubs[shift]

        def load(j, carry, pub=pub):
            s = source[j]
            d = slot[j]
            field = [pub[s, f * SUB : (f + 1) * SUB, :] for f in range(FIELDS)]
            u, n = field[0:3], field[3:6]
            both = field[7] + field[8]
            root = both * lax.rsqrt(both)
            size = u[0] * u[0] + u[1] * u[1] + u[2] * u[2]
            dot = u[0] * n[0] + u[1] * n[1] + u[2] * n[2]
            value = dot * root - field[6]
            diag_ref[d] = 1.0 - both * size
            xa[d] = value
            one_ref[d] = value
            for q in range(3):
                u_ref[d, q] = u[q]
                n_ref[d, q] = n[q]
            rho_ref[d] = field[6]
            mf_ref[d] = field[7]
            mg_ref[d] = field[8]
            p_ref[d, 0] = field[9].astype(jnp.int32)
            p_ref[d, 1] = field[10].astype(jnp.int32)
            dart = field[11].astype(jnp.int32)
            e_ref[d] = dart
            row, lane = place(dart)
            sign = jnp.where((dart & 1) == 1, -1.0, 1.0)
            for q in range(3):
                table = {r: functools.partial(lambda q, r: pub[s, q * SUB + r : q * SUB + r + 1, :], q, r) for r in range(SUB)}
                eu_ref[d, q] = sign * pick(table, row, lane)
            return carry

        lax.fori_loop(start, start + split[shift], load, 0)
        start = start + split[shift]

    lower = lax.broadcasted_iota(jnp.int32, (SUB, LANES), 1) < HALF

    def chunks(count, body):
        steps = -(-count // CHUNK)

        def step(c, carry):
            done = [body(c * CHUNK + k) for k in range(CHUNK)]
            for finish in done:
                finish()
            return carry

        if steps == 1:
            step(0, 0)
        else:
            lax.fori_loop(0, steps, step, 0)

    def table_of(i, own, ghost):
        rows = {r: functools.partial(own, i, r) for r in range(SUB)}
        for a in range(3):
            down, up = near[6 * i + 2 * a], near[6 * i + 2 * a + 1]

            def into(a=a, down=down, up=up):
                return jnp.where(lower, wide(ghost(up, 4 + a)), wide(ghost(down, 4 + a)))

            def away(a=a, down=down, up=up):
                return jnp.where(lower, wide(ghost(down, a)), wide(ghost(up, a)))

            rows[SUB + a] = into
            rows[SUB + 4 + a] = away
        return rows

    def pick_two(i, own, ghost):
        rows = table_of(i, own, ghost)
        places = [place(p_ref[i, 0]), place(p_ref[i, 1])]
        totals = [jnp.zeros((SUB, LANES), jnp.float32)] * 2
        for number, make in rows.items():
            data = wide(make())
            for end in range(2):
                row, lane = places[end]
                got = jnp.take_along_axis(data, lane, axis=1, mode="promise_in_bounds")
                totals[end] = jnp.where(row == number, got, totals[end])
        return totals

    def couple_setup(i):
        u = [u_ref[i, q] for q in range(3)]
        mf, mg = mf_ref[i], mg_ref[i]
        signs = [mf * jnp.where((p_ref[i, 0] & 1) == 1, -1.0, 1.0), -mg * jnp.where((p_ref[i, 1] & 1) == 1, -1.0, 1.0)]
        weights = [jnp.zeros((SUB, LANES), jnp.float32)] * 2
        pulls = []
        for q in range(3):
            got = pick_two(
                i, lambda i, r, q=q: u_ref[i, q, r : r + 1, :], lambda i, r, q=q: eu_ref[i, q, r : r + 1, :]
            )
            for end in range(2):
                pull = signs[end] * got[end]
                weights[end] = weights[end] + u[q] * pull
                pulls.append((end * 3 + q, pull))

        def finish():
            for at, pull in pulls:
                g_ref[i, at] = pull
            for end in range(2):
                w_ref[i, end] = weights[end]

        return finish

    chunks(counts[REACH - 1], couple_setup)

    def send_ends(x, count):
        def body(i):
            row, lane = place(e_ref[i])
            got = pick({r: functools.partial(lambda r: x[i, r : r + 1, :], r) for r in range(SUB)}, row, lane)

            def finish():
                ep_ref[i] = got

            return finish

        chunks(count, body)

    def own_of(x):
        return lambda i, r: x[i, r : r + 1, :]

    def ghost_value(i, r):
        return ep_ref[i, r : r + 1, :]

    def expand(current, following, total, reach):
        for term in range(ORDER):
            send_ends(current, counts[reach - term])

            def body(i, current=current, following=following):
                got = pick_two(i, own_of(current), ghost_value)
                value = diag_ref[i] * current[i] - w_ref[i, 0] * got[0] - w_ref[i, 1] * got[1]

                def finish():
                    following[i] = value
                    total[i] = total[i] + value

                return finish

            chunks(counts[reach - term - 1], body)
            current, following = following, current

    expand(xa, xb, one_ref, REACH)
    send_ends(one_ref, counts[ORDER + 2])

    def correct(i):
        got = pick_two(i, own_of(one_ref), ghost_value)
        both = mf_ref[i] + mg_ref[i]
        scaling = lax.rsqrt(both)
        mine = both * one_ref[i]
        length = jnp.zeros((SUB, LANES), jnp.float32)
        for q in range(3):
            part = n_ref[i, q] - scaling * (u_ref[i, q] * mine + g_ref[i, q] * got[0] + g_ref[i, 3 + q] * got[1])
            length = length + part * part
        rho = rho_ref[i]
        square = rho * rho
        value = rho - jnp.sqrt(jnp.maximum(2.0 * square - length, 0.25 * square))

        def finish():
            xa[i] = value
            two_ref[i] = value

        return finish

    chunks(counts[ORDER + 1], correct)
    expand(xa, xb, two_ref, ORDER + 1)

    def join(i):
        value = one_ref[i] + two_ref[i]

        def finish():
            xa[i] = value

        return finish

    chunks(counts[1], join)
    send_ends(xa, counts[1])

    multiplier = xa[0]
    out_mult[...] = multiplier
    first = stack_rows(bonds, 0, hold_a)
    second = stack_rows(bonds, 1, hold_b)
    small = lax.broadcasted_iota(jnp.int32, (SUB, LANES), 0)
    tall = lax.broadcasted_iota(jnp.int32, (LANES, LANES), 0)
    force = [u_ref[0, q] * multiplier for q in range(3)]
    total = jnp.zeros((3 * SUB, LANES), jnp.float32)
    zero = jnp.zeros((SUB, LANES), jnp.float32)

    def add(total, index, parts):
        hit = small == jnp.broadcast_to(index >> 7, small.shape)
        data = jnp.concatenate([jnp.where(hit, wide(part), zero) for part in parts], 0)
        hits = jnp.where(tall == jnp.broadcast_to(index & (LANES - 1), tall.shape), 1.0, 0.0)
        return total + lax.dot_general(
            data, hits, (((1,), (1,)), ((), ())), precision=lax.Precision.HIGHEST, preferred_element_type=jnp.float32
        )

    for r in range(SUB):
        total = add(total, first[r : r + 1], [force[q][r : r + 1] for q in range(3)])
        total = add(total, second[r : r + 1], [-force[q][r : r + 1] for q in range(3)])
    valid = (lax.broadcasted_iota(jnp.int32, (1, LANES), 1) & (HALF - 1)) < width
    narrow = lower[0:1]
    for a in range(3):
        down, up = near[2 * a], near[2 * a + 1]
        parts = []
        for q in range(3):
            at = 4 + a
            from_up = eu_ref[up, q, at : at + 1, :] * ep_ref[up, at : at + 1, :]
            from_down = eu_ref[down, q, at : at + 1, :] * ep_ref[down, at : at + 1, :]
            parts.append(jnp.where(valid, jnp.where(narrow, from_up, from_down), 0.0))
        total = add(total, where[a : a + 1, :], parts)
    for q in range(3):
        value = -mass[...] * total[q * SUB : (q + 1) * SUB]
        for r in range(SUB):
            out_disp[q : q + 1, r * LANES : (r + 1) * LANES] = value[r : r + 1]


def domains_near(sizes):
    def far(d, n):
        return min(d, n - d)

    ranked = sorted(
        itertools.product(*(range(n) for n in sizes)), key=lambda r: (sum(far(d, n) for d, n in zip(r, sizes)), r)
    )
    span = [sum(far(d, n) for d, n in zip(r, sizes)) for r in ranked]
    ranked = [r for r, s in zip(ranked, span) if s <= REACH]
    counts = [sum(s <= d for s in span) for d in range(REACH + 1)]
    at = {r: i for i, r in enumerate(ranked)}
    near = []
    for r in ranked:
        for a in range(3):
            for move in (-1, 1):
                to = list(r)
                to[a] = (to[a] + move) % sizes[a]
                near.append(at.get(tuple(to), 0))
    return ranked, counts, near


def per_device(old_pos, new_pos, inv_mass, rest_length, bond_pairs, live, send_index):
    sizes = [lax.axis_size(axis) for axis in AXES]
    nx, ny, nz = sizes
    atoms = old_pos.shape[1]
    width = send_index.shape[1]
    tile = (SUB, LANES)
    mass, rest, alive = (v.reshape(tile) for v in (inv_mass, rest_length, live))
    f32, i32 = jnp.float32, jnp.int32
    shape = jax.ShapeDtypeStruct

    *sent, where = pl.pallas_call(
        sent_kernel,
        out_shape=[shape(tile, f32)] * 3 + [shape(tile, i32)],
        in_specs=[VMEM] * 4,
        out_specs=[VMEM] * 4,
        scratch_shapes=[pltpu.VMEM(tile, i32)],
        name="sent",
    )(old_pos, new_pos, mass, send_index)

    arrived = []
    for axis, n, part in zip(AXES, sizes, sent):
        low = lax.ppermute(part, axis, [(i, (i + 1) % n) for i in range(n)])
        high = low if n == 2 else lax.ppermute(part, axis, [(i, (i - 1) % n) for i in range(n)])
        arrived = arrived + [low, high]

    links = pl.pallas_call(
        functools.partial(link_kernel, width),
        out_shape=shape((3 * SUB, LANES), f32),
        in_specs=[VMEM] * 4,
        out_specs=VMEM,
        scratch_shapes=[pltpu.VMEM(tile, i32), pltpu.VMEM(tile, i32), pltpu.VMEM(tile, f32)],
        cost_estimate=pl.CostEstimate(flops=4_000_000, bytes_accessed=100_000, transcendentals=0),
        name="links",
    )(bond_pairs, live.reshape(1, atoms), alive, where)

    pub = pl.pallas_call(
        functools.partial(node_kernel, width),
        out_shape=shape((FIELDS * SUB, LANES), f32),
        in_specs=[VMEM] * 13,
        out_specs=VMEM,
        scratch_shapes=[pltpu.VMEM(tile, i32), pltpu.VMEM(tile, i32), pltpu.VMEM((3 * SUB, LANES), f32)],
        name="nodes",
    )(old_pos, new_pos, mass, rest, alive, bond_pairs, links, *arrived)

    plane = ny * nz
    gathered = lax.all_to_all(jnp.broadcast_to(pub, (plane,) + pub.shape), ("gy", "gz"), 0, 0)
    parts = [gathered]
    for d in range(1, nx):
        parts.append(lax.ppermute(gathered, "gx", [(i, (i - d) % nx) for i in range(nx)]))

    ranked, counts, near = domains_near(sizes)
    order = sorted(range(len(ranked)), key=lambda i: (ranked[i][0], i))
    split = [sum(r[0] == d for r in ranked) for d in range(nx)]
    dy = jnp.asarray([ranked[i][1] for i in order], i32)
    dz = jnp.asarray([ranked[i][2] for i in order], i32)
    source = (lax.axis_index("gy") + dy) % ny * nz + (lax.axis_index("gz") + dz) % nz
    held = -(-len(ranked) // CHUNK) * CHUNK
    near = near + [0] * (6 * (held - len(ranked)))

    def keep(*lead, kind=f32):
        return pltpu.VMEM(lead + tile, kind)

    disp, mult = pl.pallas_call(
        functools.partial(main_kernel, counts, split, width),
        out_shape=[shape((3, atoms), f32), shape(tile, f32)],
        in_specs=[SMEM] * 3 + [VMEM] * (3 + nx),
        out_specs=[VMEM] * 2,
        scratch_shapes=[
            keep(held, 3), keep(held, 3), keep(held), keep(held), keep(held), keep(held, 2, kind=i32), keep(held, kind=i32),
            keep(held, 3), keep(held, 6), keep(held, 2), keep(held), keep(held), keep(held), keep(held), keep(held), keep(held),
            pltpu.VMEM(tile, i32), pltpu.VMEM(tile, i32),
        ],
        name="solve",
    )(source, jnp.asarray(order, i32), jnp.asarray(near, i32), bond_pairs, mass, where, *parts)
    return disp, mult.reshape(atoms)


def solution(mesh):
    flat = P(AXES)
    rows = P(None, AXES)
    return jax.shard_map(
        per_device,
        mesh=mesh,
        in_specs=(rows, rows, flat, flat, rows, flat, P(AXES, None)),
        out_specs=(rows, flat),
        check_vma=False,
    )
```

profile of v0, /device:TPU:0, one launch (start us, length us, event | category | flops | bytes accessed | tf_op | source)
XLA Modules:
  0.0 79.5 jit_solution(14163174147548959725)
XLA Ops:
  0.6 1.6 %sent.1 = (f32[8,128]{1,0:T(8,128)}, f32[8,128]{1,0:T(8,128)}, f32[8,128]{1,0:T(8,128)}, s32[8,128]{1,0:T(8,128)}) custom-call(f32[3,1024]{1,0:T(4,128)} %old.3, f32[3,1024]{1,0:T(4,128)} %new.3, f32[8,128]{1,0:T(8,128)} %bitcast.5, s32[6,48]{1,0:T(8,128)} %send.1), custom_call_target="tpu_custom_call" | custom-call | tf_op jit(solution)/shard_map/sent/pallas_call | solution.py:439
  2.2 0.0 copy-start.8
  2.2 0.5 collective-permute-start
  2.7 2.5 %collective-permute-start.1 = (f32[8,128]{1,0:T(8,128)}, f32[8,128]{1,0:T(8,128)S(1)}, u32[]{:S(2)}, u32[]{:S(2)}) collective-permute-start(f32[8,128]{1,0:T(8,128)} %get-tuple-element.10), channel_id=1, source_target_pairs={{0,8},{8,0},{1,9},{9,1},{2,10},{10,2},{3,11},{11,3},{4,12},{12,4},... | collective-permute-start | bytes 12296 | tf_op jit(solution)/shard_map/ppermute | solution.py:450
  5.2 0.0 copy-done.8
  5.2 4.6 %collective-permute-start.3 = (f32[8,128]{1,0:T(8,128)S(1)}, f32[8,128]{1,0:T(8,128)S(1)}, u32[]{:S(2)}, u32[]{:S(2)}) collective-permute-start(f32[8,128]{1,0:T(8,128)S(1)} %copy-done.8), channel_id=1, source_target_pairs={{0,7},{1,0},{2,1},{3,2},{4,3},{5,4},{6,5},{7,6},{8,15},{9,8},{10,9... | collective-permute-start | bytes 12296 | tf_op jit(solution)/shard_map/ppermute | solution.py:451
  9.8 0.0 collective-permute-start.2
  9.8 1.9 %links.1 = f32[24,128]{1,0:T(8,128)} custom-call(s32[2,1024]{1,0:T(2,128)} %bonds.5, s32[1,1024]{1,0:T(1,128)} %bitcast.9, s32[8,128]{1,0:T(8,128)} %bitcast.8, s32[8,128]{1,0:T(8,128)} %get-tuple-element.8.where), custom_call_target="tpu_custom_call" | custom-call | flops 4000000 | bytes 100000 | tf_op jit(solution)/shard_map/links/pallas_call | solution.py:454
  11.6 0.0 collective-permute-done.refs_0_.refs_1_
  11.6 0.0 copy-start.2
  11.7 0.0 collective-permute-done.1.refs_2_.refs_3_
  11.7 0.0 copy-start.3
  11.7 0.0 collective-permute-done.3.refs_5_
  11.7 0.0 copy-start.4
  11.7 4.4 %collective-permute-done.2.refs_4_ = f32[8,128]{1,0:T(8,128)S(1)} collective-permute-done((f32[8,128]{1,0:T(8,128)S(1)}, f32[8,128]{1,0:T(8,128)S(1)}, u32[]{:S(2)}, u32[]{:S(2)}) %collective-permute-start.2) | collective-permute-done | bytes 4128 | tf_op jit(solution)/shard_map/ppermute | solution.py:450
  16.1 0.0 copy-start.5
  16.1 0.0 copy-done.2
  16.1 0.0 copy-done.3
  16.1 0.0 copy-done.4
  16.1 0.6 copy-done.5
  16.7 1.7 %nodes.1 = f32[96,128]{1,0:T(8,128)} custom-call(f32[3,1024]{1,0:T(4,128)} %old.3, f32[3,1024]{1,0:T(4,128)} %new.3, f32[8,128]{1,0:T(8,128)} %bitcast.6, f32[8,128]{1,0:T(8,128)} %bitcast.11, s32[8,128]{1,0:T(8,128)} %bitcast.10, s32[2,1024]{1,0:T(2,128)} %bonds.5, f32[24,128]{1,0:T(8,128)} %links.1, f32[8,128]{1,0:T(8,128)} %copy-done.2, ...), custom_call_target="tpu_custom_call" | custom-call | tf_op jit(solution)/shard_map/nodes/pallas_call | solution.py:464
  18.4 0.9 %broadcast_in_dim.3 = f32[16,96,128]{2,1,0:T(8,128)S(1)} broadcast(f32[96,128]{1,0:T(8,128)} %nodes.1), dimensions={1,2} | broadcast | bytes 835584 | tf_op jit(solution)/shard_map/broadcast_in_dim | solution.py:474
  19.3 23.0 %all_to_all.5.refs_0_ = f32[16,96,128]{2,1,0:T(8,128)S(1)} all-to-all(f32[16,96,128]{2,1,0:T(8,128)S(1)} %broadcast_in_dim.3), channel_id=1, replica_groups=mesh['gx'=2,'gy'=2,'gz'=8] {'gy','gz'}, dimensions={0} | all-to-all | bytes 1572864 | tf_op jit(solution)/shard_map/all_to_all | solution.py:474
  42.3 0.0 copy-start
  42.3 0.0 collective-permute-start.4
  42.3 0.0 copy-start.6
  42.3 0.0 copy-start.7
  42.3 0.6 copy-done.6
  43.0 0.1 copy-done.7
  43.0 0.6 fusion.source
  43.6 1.0 %collective-permute-done.4.refs_1_ = f32[16,96,128]{2,1,0:T(8,128)S(1)} collective-permute-done((f32[16,96,128]{2,1,0:T(8,128)S(1)}, f32[16,96,128]{2,1,0:T(8,128)S(1)}, u32[]{:S(2)}, u32[]{:S(2)}) %collective-permute-start.4) | collective-permute-done | bytes 786464 | tf_op jit(solution)/shard_map/ppermute | solution.py:477
  44.6 0.0 copy-done
  44.6 0.0 copy-start.1
  44.6 0.9 %copy-done.1 = f32[16,96,128]{2,1,0:T(8,128)} copy-done((f32[16,96,128]{2,1,0:T(8,128)}, f32[16,96,128]{2,1,0:T(8,128)S(1)}, u32[]{:S(2)}) %copy-start.1) | copy-done | bytes 786456
  45.5 34.0 %solve.1 = (f32[3,1024]{1,0:T(4,128)}, f32[8,128]{1,0:T(8,128)}) custom-call(s32[32]{0:T(128)} %fusion.source, s32[32]{0:T(128)} %constant.46.clone.slot, s32[192]{0:T(256)} %constant.47.clone.near, s32[2,1024]{1,0:T(2,128)} %bonds.5, f32[8,128]{1,0:T(8,128)} %bitcast.7, s32[8,128]{1,0:T(8,128)} %get-tuple-element.8.where, f32[16,96,128]{2,1,0:T(8,128)} %copy-done, ...), custom_call_target="tpu_custom_call" | custom-call | tf_op jit(solution)/shard_map/solve/pallas_call | solution.py:491
Async XLA Ops:
  2.2 3.0 %copy-start.8 = (f32[8,128]{1,0:T(8,128)S(1)}, f32[8,128]{1,0:T(8,128)}, u32[]{:S(2)}) copy-start(f32[8,128]{1,0:T(8,128)} %get-tuple-element.11) | copy-start | bytes 12292
  2.2 9.5 %collective-permute-start = (f32[8,128]{1,0:T(8,128)}, f32[8,128]{1,0:T(8,128)S(1)}, u32[]{:S(2)}, u32[]{:S(2)}) collective-permute-start(f32[8,128]{1,0:T(8,128)} %get-tuple-element.9), channel_id=1, source_target_pairs={{0,16},{16,0},{1,17},{17,1},{2,18},{18,2},{3,19},{19,3},{4,20},{20... | collective-permute-start | bytes 12296 | tf_op jit(solution)/shard_map/ppermute | solution.py:450
  2.7 9.0 %collective-permute-start.1 = (f32[8,128]{1,0:T(8,128)}, f32[8,128]{1,0:T(8,128)S(1)}, u32[]{:S(2)}, u32[]{:S(2)}) collective-permute-start(f32[8,128]{1,0:T(8,128)} %get-tuple-element.10), channel_id=1, source_target_pairs={{0,8},{8,0},{1,9},{9,1},{2,10},{10,2},{3,11},{11,3},{4,12},{12,4},... | collective-permute-start | bytes 12296 | tf_op jit(solution)/shard_map/ppermute | solution.py:450
  5.2 6.4 %collective-permute-start.3 = (f32[8,128]{1,0:T(8,128)S(1)}, f32[8,128]{1,0:T(8,128)S(1)}, u32[]{:S(2)}, u32[]{:S(2)}) collective-permute-start(f32[8,128]{1,0:T(8,128)S(1)} %copy-done.8), channel_id=1, source_target_pairs={{0,7},{1,0},{2,1},{3,2},{4,3},{5,4},{6,5},{7,6},{8,15},{9,8},{10,9... | collective-permute-start | bytes 12296 | tf_op jit(solution)/shard_map/ppermute | solution.py:451
  9.8 6.3 %collective-permute-start.2 = (f32[8,128]{1,0:T(8,128)S(1)}, f32[8,128]{1,0:T(8,128)S(1)}, u32[]{:S(2)}, u32[]{:S(2)}) collective-permute-start(f32[8,128]{1,0:T(8,128)S(1)} %copy-done.8), channel_id=1, source_target_pairs={{0,1},{1,2},{2,3},{3,4},{4,5},{5,6},{6,7},{7,0},{8,9},{9,10},{10,1... | collective-permute-start | bytes 12296 | tf_op jit(solution)/shard_map/ppermute | solution.py:450
  11.6 4.5 %copy-start.2 = (f32[8,128]{1,0:T(8,128)}, f32[8,128]{1,0:T(8,128)S(1)}, u32[]{:S(2)}) copy-start(f32[8,128]{1,0:T(8,128)S(1)} %collective-permute-done.refs_0_.refs_1_) | copy-start | bytes 12292
  11.7 4.4 %copy-start.3 = (f32[8,128]{1,0:T(8,128)}, f32[8,128]{1,0:T(8,128)S(1)}, u32[]{:S(2)}) copy-start(f32[8,128]{1,0:T(8,128)S(1)} %collective-permute-done.1.refs_2_.refs_3_) | copy-start | bytes 12292
  11.7 4.4 %copy-start.4 = (f32[8,128]{1,0:T(8,128)}, f32[8,128]{1,0:T(8,128)S(1)}, u32[]{:S(2)}) copy-start(f32[8,128]{1,0:T(8,128)S(1)} %collective-permute-done.3.refs_5_) | copy-start | bytes 12292
  16.1 0.6 copy-start.5
  42.3 2.3 %copy-start = (f32[16,96,128]{2,1,0:T(8,128)}, f32[16,96,128]{2,1,0:T(8,128)S(1)}, u32[]{:S(2)}) copy-start(f32[16,96,128]{2,1,0:T(8,128)S(1)} %all_to_all.5.refs_0_) | copy-start | bytes 2359300
  42.3 2.3 %collective-permute-start.4 = (f32[16,96,128]{2,1,0:T(8,128)S(1)}, f32[16,96,128]{2,1,0:T(8,128)S(1)}, u32[]{:S(2)}, u32[]{:S(2)}) collective-permute-start(f32[16,96,128]{2,1,0:T(8,128)S(1)} %all_to_all.5.refs_0_), channel_id=1, source_target_pairs={{0,16},{16,0},{1,17},{17,1},{2,18},{18,2},{3,19},{19,3},{4,20},{20... | collective-permute-start | bytes 2359304 | tf_op jit(solution)/shard_map/ppermute | solution.py:477
  42.3 0.7 copy-start.6
  42.3 0.7 copy-start.7
  44.6 0.9 %copy-start.1 = (f32[16,96,128]{2,1,0:T(8,128)}, f32[16,96,128]{2,1,0:T(8,128)S(1)}, u32[]{:S(2)}) copy-start(f32[16,96,128]{2,1,0:T(8,128)S(1)} %collective-permute-done.4.refs_1_) | copy-start | bytes 2359300
where the time goes:
time: 79.9 us; the launch traced here: 79.5 us
  Pallas kernels  39.1 us (49%)
  blocking collectives  23 us (29%)
  starting transfers between devices  7.6 us (10%)
  waiting for transfers between devices  5.38 us (7%)
  local copies, waits for them, and re-layouts  3.1 us (4%)
    pallas_call x1, Pallas kernels, per_device(): pl.pallas_call(functools.partial(main_kernel, counts, split, width), out_...  34 us
    all_to_all x1, blocking collectives, per_device(): lax.all_to_all(jnp.broadcast_to(pub, (plane,) + pub.shape), ('gy', 'gz'),...  23 us
    ppermute x1, starting transfers between devices, per_device(): lax.ppermute(part, axis, [(i, (i - 1) % n) for i in range(n)])  4.56 us
    ppermute x3, waiting for transfers between devices, per_device(): low = lax.ppermute(part, axis, [(i, (i + 1) % n) for i in range(n)])  4.41 us
    ppermute x3, starting transfers between devices, per_device(): low = lax.ppermute(part, axis, [(i, (i + 1) % n) for i in range(n)])  3.04 us
    unnamed x18, local copies, waits for them, and re-layouts  2.24 us
    pallas_call x1, Pallas kernels, per_device(): pl.pallas_call(functools.partial(link_kernel, width), out_shape=shape((3...  1.85 us
    pallas_call x1, Pallas kernels, per_device(): pl.pallas_call(functools.partial(node_kernel, width), out_shape=shape((FI...  1.71 us
  transfers between devices with their start and end apart: 5, of which 2 were waited for; matrix products, arithmetic and copies ran while one was open for 1% of the time, Pallas kernels for 2%

commit v1 on v0

--- a/solution.py
+++ b/solution.py
@@ -1,5 +1,6 @@
 import functools
 import itertools
+import math
 
 import jax
 import jax.numpy as jnp
@@ -14,7 +15,8 @@
 LANES = 128
 HALF = LANES // 2
 SUB = 8
-CHUNK = 8
+CHUNK = 16
+LOAD = 4
 FIELDS = 12
 REACH = 2 * (ORDER + 1)
 VMEM = pl.BlockSpec(memory_space=pltpu.VMEM)
@@ -195,7 +197,7 @@
     for shift in range(shifts):
         pub = pubs[shift]
 
-        def load(j, carry, pub=pub):
+        def load(j, pub=pub):
             s = source[j]
             d = slot[j]
             field = [pub[s, f * SUB : (f + 1) * SUB, :] for f in range(FIELDS)]
@@ -205,27 +207,39 @@
             size = u[0] * u[0] + u[1] * u[1] + u[2] * u[2]
             dot = u[0] * n[0] + u[1] * n[1] + u[2] * n[2]
             value = dot * root - field[6]
-            diag_ref[d] = 1.0 - both * size
-            xa[d] = value
-            one_ref[d] = value
-            for q in range(3):
-                u_ref[d, q] = u[q]
-                n_ref[d, q] = n[q]
-            rho_ref[d] = field[6]
-            mf_ref[d] = field[7]
-            mg_ref[d] = field[8]
-            p_ref[d, 0] = field[9].astype(jnp.int32)
-            p_ref[d, 1] = field[10].astype(jnp.int32)
             dart = field[11].astype(jnp.int32)
-            e_ref[d] = dart
             row, lane = place(dart)
             sign = jnp.where((dart & 1) == 1, -1.0, 1.0)
+            ends = []
             for q in range(3):
                 table = {r: functools.partial(lambda q, r: pub[s, q * SUB + r : q * SUB + r + 1, :], q, r) for r in range(SUB)}
-                eu_ref[d, q] = sign * pick(table, row, lane)
+                ends.append(sign * pick(table, row, lane))
+
+            def finish():
+                diag_ref[d] = 1.0 - both * size
+                xa[d] = value
+                one_ref[d] = value
+                for q in range(3):
+                    u_ref[d, q] = u[q]
+                    n_ref[d, q] = n[q]
+                    eu_ref[d, q] = ends[q]
+                rho_ref[d] = field[6]
+                mf_ref[d] = field[7]
+                mg_ref[d] = field[8]
+                p_ref[d, 0] = field[9].astype(jnp.int32)
+                p_ref[d, 1] = field[10].astype(jnp.int32)
+                e_ref[d] = dart
+
+            return finish
+
+        unroll = math.gcd(LOAD, split[shift])
+
+        def loads(c, carry, load=load, start=start, unroll=unroll):
+            for finish in [load(start + c * unroll + k) for k in range(unroll)]:
+                finish()
             return carry
 
-        lax.fori_loop(start, start + split[shift], load, 0)
+        lax.fori_loop(0, split[shift] // unroll, loads, 0)
         start = start + split[shift]
 
     lower = lax.broadcasted_iota(jnp.int32, (SUB, LANES), 1) < HALF
@@ -259,17 +273,26 @@
             rows[SUB + 4 + a] = away
         return rows
 
+    def pick_ends(i, tables):
+        loaded = [{number: wide(make()) for number, make in table.items()} for table in tables]
+        results = []
+        for end in range(2):
+            row, lane = place(p_ref[i, end])
+            seen = [number for number in loaded[0] if end == 1 or number < SUB + 4]
+            hits = {number: row == number for number in seen}
+            got = []
+            for data in loaded:
+                total = jnp.zeros((SUB, LANES), jnp.float32)
+                for number in seen:
+                    value = jnp.take_along_axis(data[number], lane, axis=1, mode="promise_in_bounds")
+                    total = jnp.where(hits[number], value, total)
+                got.append(total)
+            results.append(got)
+        return results
+
     def pick_two(i, own, ghost):
-        rows = table_of(i, own, ghost)
-        places = [place(p_ref[i, 0]), place(p_ref[i, 1])]
-        totals = [jnp.zeros((SUB, LANES), jnp.float32)] * 2
-        for number, make in rows.items():
-            data = wide(make())
-            for end in range(2):
-                row, lane = places[end]
-                got = jnp.take_along_axis(data, lane, axis=1, mode="promise_in_bounds")
-                totals[end] = jnp.where(row == number, got, totals[end])
-        return totals
+        one, two = pick_ends(i, [table_of(i, own, ghost)])
+        return one[0], two[0]
 
     def couple_setup(i):
         u = [u_ref[i, q] for q in range(3)]
@@ -277,12 +300,13 @@
         signs = [mf * jnp.where((p_ref[i, 0] & 1) == 1, -1.0, 1.0), -mg * jnp.where((p_ref[i, 1] & 1) == 1, -1.0, 1.0)]
         weights = [jnp.zeros((SUB, LANES), jnp.float32)] * 2
         pulls = []
-        for q in range(3):
-            got = pick_two(
-                i, lambda i, r, q=q: u_ref[i, q, r : r + 1, :], lambda i, r, q=q: eu_ref[i, q, r : r + 1, :]
-            )
-            for end in range(2):
-                pull = signs[end] * got[end]
+        tables = [
+            table_of(i, lambda i, r, q=q: u_ref[i, q, r : r + 1, :], lambda i, r, q=q: eu_ref[i, q, r : r + 1, :])
+            for q in range(3)
+        ]
+        for end, got in enumerate(pick_ends(i, tables)):
+            for q in range(3):
+                pull = signs[end] * got[q]
                 weights[end] = weights[end] + u[q] * pull
                 pulls.append((end * 3 + q, pull))
 

time: 79.9 us -> 68.8 us (0.86)
  Pallas kernels: 39.1 us -> 28 us
    pallas_call x1, Pallas kernels: 34 us -> 22.9 us  [per_device(): pl.pallas_call(functools.partial(main_kernel, counts, split, width), out_...]
  transfers between devices with their start and end apart: 5 -> 5, of which waited for: 2 -> 2; matrix products, arithmetic and copies ran while one was open for 1% -> 1% of each run, Pallas kernels for 2% -> 3%
where the time goes in v1:
time: 68.8 us; the launch traced here: 68.4 us
  Pallas kernels  28 us (41%)
  blocking collectives  23 us (33%)
  starting transfers between devices  7.6 us (11%)
  waiting for transfers between devices  5.38 us (8%)
  local copies, waits for them, and re-layouts  3.1 us (5%)
  between operations  0.69 us (1%)
    all_to_all x1, blocking collectives, per_device(): lax.all_to_all(jnp.broadcast_to(pub, (plane,) + pub.shape), ('gy', 'gz'),...  23 us
    pallas_call x1, Pallas kernels, per_device(): pl.pallas_call(functools.partial(main_kernel, counts, split, width), out_...  22.9 us
    ppermute x1, starting transfers between devices, per_device(): lax.ppermute(part, axis, [(i, (i - 1) % n) for i in range(n)])  4.56 us
    ppermute x3, waiting for transfers between devices, per_device(): low = lax.ppermute(part, axis, [(i, (i + 1) % n) for i in range(n)])  4.41 us
    ppermute x3, starting transfers between devices, per_device(): low = lax.ppermute(part, axis, [(i, (i + 1) % n) for i in range(n)])  3.04 us
    unnamed x18, local copies, waits for them, and re-layouts  2.24 us
    pallas_call x1, Pallas kernels, per_device(): pl.pallas_call(functools.partial(link_kernel, width), out_shape=shape((3...  1.85 us
    pallas_call x1, Pallas kernels, per_device(): pl.pallas_call(functools.partial(node_kernel, width), out_shape=shape((FI...  1.71 us
  transfers between devices with their start and end apart: 5, of which 2 were waited for; matrix products, arithmetic and copies ran while one was open for 1% of the time, Pallas kernels for 3%

profile of v1, /device:TPU:0, one launch (start us, length us, event | category | flops | bytes accessed | tf_op | source)
XLA Modules:
  0.0 68.4 jit_solution(5407497851149029506)
XLA Ops:
  0.6 1.6 %sent.1 = (f32[8,128]{1,0:T(8,128)}, f32[8,128]{1,0:T(8,128)}, f32[8,128]{1,0:T(8,128)}, s32[8,128]{1,0:T(8,128)}) custom-call(f32[3,1024]{1,0:T(4,128)} %old.3, f32[3,1024]{1,0:T(4,128)} %new.3, f32[8,128]{1,0:T(8,128)} %bitcast.5, s32[6,48]{1,0:T(8,128)} %send.1), custom_call_target="tpu_custom_call" | custom-call | tf_op jit(solution)/shard_map/sent/pallas_call | solution.py:463
  2.2 0.0 copy-start.8
  2.2 0.5 collective-permute-start
  2.7 2.5 %collective-permute-start.1 = (f32[8,128]{1,0:T(8,128)}, f32[8,128]{1,0:T(8,128)S(1)}, u32[]{:S(2)}, u32[]{:S(2)}) collective-permute-start(f32[8,128]{1,0:T(8,128)} %get-tuple-element.10), channel_id=1, source_target_pairs={{0,8},{8,0},{1,9},{9,1},{2,10},{10,2},{3,11},{11,3},{4,12},{12,4},... | collective-permute-start | bytes 12296 | tf_op jit(solution)/shard_map/ppermute | solution.py:474
  5.2 0.0 copy-done.8
  5.2 4.6 %collective-permute-start.3 = (f32[8,128]{1,0:T(8,128)S(1)}, f32[8,128]{1,0:T(8,128)S(1)}, u32[]{:S(2)}, u32[]{:S(2)}) collective-permute-start(f32[8,128]{1,0:T(8,128)S(1)} %copy-done.8), channel_id=1, source_target_pairs={{0,7},{1,0},{2,1},{3,2},{4,3},{5,4},{6,5},{7,6},{8,15},{9,8},{10,9... | collective-permute-start | bytes 12296 | tf_op jit(solution)/shard_map/ppermute | solution.py:475
  9.8 0.0 collective-permute-start.2
  9.8 1.9 %links.1 = f32[24,128]{1,0:T(8,128)} custom-call(s32[2,1024]{1,0:T(2,128)} %bonds.5, s32[1,1024]{1,0:T(1,128)} %bitcast.9, s32[8,128]{1,0:T(8,128)} %bitcast.8, s32[8,128]{1,0:T(8,128)} %get-tuple-element.8.where), custom_call_target="tpu_custom_call" | custom-call | flops 4000000 | bytes 100000 | tf_op jit(solution)/shard_map/links/pallas_call | solution.py:478
  11.6 0.0 collective-permute-done.refs_0_.refs_1_
  11.6 0.0 copy-start.2
  11.7 0.0 collective-permute-done.1.refs_2_.refs_3_
  11.7 0.0 copy-start.3
  11.7 0.0 collective-permute-done.3.refs_5_
  11.7 0.0 copy-start.4
  11.7 4.4 %collective-permute-done.2.refs_4_ = f32[8,128]{1,0:T(8,128)S(1)} collective-permute-done((f32[8,128]{1,0:T(8,128)S(1)}, f32[8,128]{1,0:T(8,128)S(1)}, u32[]{:S(2)}, u32[]{:S(2)}) %collective-permute-start.2) | collective-permute-done | bytes 4128 | tf_op jit(solution)/shard_map/ppermute | solution.py:474
  16.1 0.0 copy-start.5
  16.1 0.0 copy-done.2
  16.1 0.0 copy-done.3
  16.1 0.0 copy-done.4
  16.1 0.6 copy-done.5
  16.7 1.7 %nodes.1 = f32[96,128]{1,0:T(8,128)} custom-call(f32[3,1024]{1,0:T(4,128)} %old.3, f32[3,1024]{1,0:T(4,128)} %new.3, f32[8,128]{1,0:T(8,128)} %bitcast.6, f32[8,128]{1,0:T(8,128)} %bitcast.11, s32[8,128]{1,0:T(8,128)} %bitcast.10, s32[2,1024]{1,0:T(2,128)} %bonds.5, f32[24,128]{1,0:T(8,128)} %links.1, f32[8,128]{1,0:T(8,128)} %copy-done.2, ...), custom_call_target="tpu_custom_call" | custom-call | tf_op jit(solution)/shard_map/nodes/pallas_call | solution.py:488
  18.4 0.9 %broadcast_in_dim.3 = f32[16,96,128]{2,1,0:T(8,128)S(1)} broadcast(f32[96,128]{1,0:T(8,128)} %nodes.1), dimensions={1,2} | broadcast | bytes 835584 | tf_op jit(solution)/shard_map/broadcast_in_dim | solution.py:498
  19.3 23.0 %all_to_all.5.refs_0_ = f32[16,96,128]{2,1,0:T(8,128)S(1)} all-to-all(f32[16,96,128]{2,1,0:T(8,128)S(1)} %broadcast_in_dim.3), channel_id=1, replica_groups=mesh['gx'=2,'gy'=2,'gz'=8] {'gy','gz'}, dimensions={0} | all-to-all | bytes 1572864 | tf_op jit(solution)/shard_map/all_to_all | solution.py:498
  42.3 0.0 copy-start
  42.3 0.0 collective-permute-start.4
  42.3 0.0 copy-start.6
  42.3 0.0 copy-start.7
  42.3 0.6 copy-done.6
  43.0 0.1 copy-done.7
  43.0 0.6 fusion.source
  43.6 1.0 %collective-permute-done.4.refs_1_ = f32[16,96,128]{2,1,0:T(8,128)S(1)} collective-permute-done((f32[16,96,128]{2,1,0:T(8,128)S(1)}, f32[16,96,128]{2,1,0:T(8,128)S(1)}, u32[]{:S(2)}, u32[]{:S(2)}) %collective-permute-start.4) | collective-permute-done | bytes 786464 | tf_op jit(solution)/shard_map/ppermute | solution.py:501
  44.6 0.0 copy-done
  44.6 0.0 copy-start.1
  44.6 0.9 %copy-done.1 = f32[16,96,128]{2,1,0:T(8,128)} copy-done((f32[16,96,128]{2,1,0:T(8,128)}, f32[16,96,128]{2,1,0:T(8,128)S(1)}, u32[]{:S(2)}) %copy-start.1) | copy-done | bytes 786456
  45.5 22.9 %solve.1 = (f32[3,1024]{1,0:T(4,128)}, f32[8,128]{1,0:T(8,128)}) custom-call(s32[32]{0:T(128)} %fusion.source, s32[32]{0:T(128)} %constant.46.clone.slot, s32[192]{0:T(256)} %constant.47.clone.near, s32[2,1024]{1,0:T(2,128)} %bonds.5, f32[8,128]{1,0:T(8,128)} %bitcast.7, s32[8,128]{1,0:T(8,128)} %get-tuple-element.8.where, f32[16,96,128]{2,1,0:T(8,128)} %copy-done, ...), custom_call_target="tpu_custom_call" | custom-call | tf_op jit(solution)/shard_map/solve/pallas_call | solution.py:515
Async XLA Ops:
  2.2 3.0 %copy-start.8 = (f32[8,128]{1,0:T(8,128)S(1)}, f32[8,128]{1,0:T(8,128)}, u32[]{:S(2)}) copy-start(f32[8,128]{1,0:T(8,128)} %get-tuple-element.11) | copy-start | bytes 12292
  2.2 9.5 %collective-permute-start = (f32[8,128]{1,0:T(8,128)}, f32[8,128]{1,0:T(8,128)S(1)}, u32[]{:S(2)}, u32[]{:S(2)}) collective-permute-start(f32[8,128]{1,0:T(8,128)} %get-tuple-element.9), channel_id=1, source_target_pairs={{0,16},{16,0},{1,17},{17,1},{2,18},{18,2},{3,19},{19,3},{4,20},{20... | collective-permute-start | bytes 12296 | tf_op jit(solution)/shard_map/ppermute | solution.py:474
  2.7 9.0 %collective-permute-start.1 = (f32[8,128]{1,0:T(8,128)}, f32[8,128]{1,0:T(8,128)S(1)}, u32[]{:S(2)}, u32[]{:S(2)}) collective-permute-start(f32[8,128]{1,0:T(8,128)} %get-tuple-element.10), channel_id=1, source_target_pairs={{0,8},{8,0},{1,9},{9,1},{2,10},{10,2},{3,11},{11,3},{4,12},{12,4},... | collective-permute-start | bytes 12296 | tf_op jit(solution)/shard_map/ppermute | solution.py:474
  5.2 6.4 %collective-permute-start.3 = (f32[8,128]{1,0:T(8,128)S(1)}, f32[8,128]{1,0:T(8,128)S(1)}, u32[]{:S(2)}, u32[]{:S(2)}) collective-permute-start(f32[8,128]{1,0:T(8,128)S(1)} %copy-done.8), channel_id=1, source_target_pairs={{0,7},{1,0},{2,1},{3,2},{4,3},{5,4},{6,5},{7,6},{8,15},{9,8},{10,9... | collective-permute-start | bytes 12296 | tf_op jit(solution)/shard_map/ppermute | solution.py:475
  9.8 6.3 %collective-permute-start.2 = (f32[8,128]{1,0:T(8,128)S(1)}, f32[8,128]{1,0:T(8,128)S(1)}, u32[]{:S(2)}, u32[]{:S(2)}) collective-permute-start(f32[8,128]{1,0:T(8,128)S(1)} %copy-done.8), channel_id=1, source_target_pairs={{0,1},{1,2},{2,3},{3,4},{4,5},{5,6},{6,7},{7,0},{8,9},{9,10},{10,1... | collective-permute-start | bytes 12296 | tf_op jit(solution)/shard_map/ppermute | solution.py:474
  11.6 4.5 %copy-start.2 = (f32[8,128]{1,0:T(8,128)}, f32[8,128]{1,0:T(8,128)S(1)}, u32[]{:S(2)}) copy-start(f32[8,128]{1,0:T(8,128)S(1)} %collective-permute-done.refs_0_.refs_1_) | copy-start | bytes 12292
  11.7 4.4 %copy-start.3 = (f32[8,128]{1,0:T(8,128)}, f32[8,128]{1,0:T(8,128)S(1)}, u32[]{:S(2)}) copy-start(f32[8,128]{1,0:T(8,128)S(1)} %collective-permute-done.1.refs_2_.refs_3_) | copy-start | bytes 12292
  11.7 4.4 %copy-start.4 = (f32[8,128]{1,0:T(8,128)}, f32[8,128]{1,0:T(8,128)S(1)}, u32[]{:S(2)}) copy-start(f32[8,128]{1,0:T(8,128)S(1)} %collective-permute-done.3.refs_5_) | copy-start | bytes 12292
  16.1 0.6 copy-start.5
  42.3 2.3 %copy-start = (f32[16,96,128]{2,1,0:T(8,128)}, f32[16,96,128]{2,1,0:T(8,128)S(1)}, u32[]{:S(2)}) copy-start(f32[16,96,128]{2,1,0:T(8,128)S(1)} %all_to_all.5.refs_0_) | copy-start | bytes 2359300
  42.3 2.3 %collective-permute-start.4 = (f32[16,96,128]{2,1,0:T(8,128)S(1)}, f32[16,96,128]{2,1,0:T(8,128)S(1)}, u32[]{:S(2)}, u32[]{:S(2)}) collective-permute-start(f32[16,96,128]{2,1,0:T(8,128)S(1)} %all_to_all.5.refs_0_), channel_id=1, source_target_pairs={{0,16},{16,0},{1,17},{17,1},{2,18},{18,2},{3,19},{19,3},{4,20},{20... | collective-permute-start | bytes 2359304 | tf_op jit(solution)/shard_map/ppermute | solution.py:501
  42.3 0.7 copy-start.6
  42.3 0.7 %copy-start.7 = (s32[32]{0:T(128)S(1)}, s32[32]{0:T(128)}, u32[]{:S(2)}) copy-start(s32[32]{0:T(128)} %constant.44.clone) | copy-start | bytes 388
  44.6 0.9 %copy-start.1 = (f32[16,96,128]{2,1,0:T(8,128)}, f32[16,96,128]{2,1,0:T(8,128)S(1)}, u32[]{:S(2)}) copy-start(f32[16,96,128]{2,1,0:T(8,128)S(1)} %collective-permute-done.4.refs_1_) | copy-start | bytes 2359300

commit v2 on v1

v2 whole, which is shorter than its diff:
```python
import functools
import itertools

import jax
import jax.numpy as jnp
import numpy as np
from jax import lax
from jax.experimental import pallas as pl
from jax.experimental.pallas import tpu as pltpu
from jax.sharding import PartitionSpec as P

ORDER = 4
AXES = ("gx", "gy", "gz")
LANES = 128
HALF = LANES // 2
SUB = 8
CHUNK = 16
LOAD = 4
FIELDS = 12
REACH = 2 * (ORDER + 1)
VMEM = pl.BlockSpec(memory_space=pltpu.VMEM)


def wide(row):
    return jnp.broadcast_to(row, (SUB, LANES))


def pick(tables, row, lane):
    total = jnp.zeros((SUB, LANES), jnp.float32)
    for number, load in tables.items():
        got = jnp.take_along_axis(wide(load()), lane, axis=1, mode="promise_in_bounds")
        total = jnp.where(row == number, got.astype(jnp.float32), total)
    return total


def flat_rows(ref, q):
    return {r: functools.partial(lambda q, r: ref[q : q + 1, r * LANES : (r + 1) * LANES], q, r) for r in range(SUB)}


def tile_rows(ref, base=0):
    return {r: functools.partial(lambda r: ref[base + r : base + r + 1, :], r) for r in range(SUB)}


def stack_rows(ref, q, hold):
    for r in range(SUB):
        hold[r : r + 1, :] = ref[q : q + 1, r * LANES : (r + 1) * LANES]
    return hold[...]


def second_place(second, width):
    atoms = SUB * LANES
    slot = second - atoms
    block = jnp.zeros_like(second)
    for b in range(1, 6):
        block = block + (slot >= b * width).astype(jnp.int32)
    lane = slot - block * width + (block & 1) * HALF
    remote = second >= atoms
    row = jnp.where(remote, 12 + (block >> 1), second >> 7)
    return row, jnp.where(remote, lane, second & (LANES - 1))


def nt_dot(a, b):
    return lax.dot_general(a, b, (((1,), (1,)), ((), ())), preferred_element_type=jnp.float32)


def split_codes(hit, code):
    code = jnp.broadcast_to(code, hit.shape)
    zero = jnp.zeros_like(code)
    both = jnp.concatenate([jnp.where(hit, code >> 4, zero), jnp.where(hit, code & 15, zero)], 0)
    return both.astype(jnp.float32).astype(jnp.bfloat16)


def lane_hits(lane, count):
    hits = lax.broadcasted_iota(jnp.int32, (LANES, count), 0) == jnp.broadcast_to(lane, (LANES, count))
    return jnp.where(hits, 1.0, 0.0).astype(jnp.bfloat16)


def publish_kernel(width, old, new, mass, rest, live, live_row, bonds, send, pub, own, pad, hold_a, hold_b, s_ref, row_ref):
    atoms = SUB * LANES
    sublane = lax.broadcasted_iota(jnp.int32, (SUB, LANES), 0)
    spot = lax.broadcasted_iota(jnp.int32, (SUB, LANES), 1)
    lanes = spot[0:1]

    pad[...] = jnp.zeros_like(pad)
    pad[0:6, 0:width] = send[...]
    low = pad[...]
    high = pltpu.roll(low, HALF, 1)
    ones = [low[2 * a : 2 * a + 1] + high[2 * a + 1 : 2 * a + 2] for a in range(3)]
    for a in range(3):
        pad[a : a + 1, :] = ones[a]
    index = pad[...]
    index = jnp.where(sublane < 3, index, 0)
    sent_place = (index >> 7, index & (LANES - 1))

    first_row = bonds[0:1, :]
    second_row = bonds[1:2, :]
    usable = (live_row[...] != 0) & (first_row != second_row)
    node = lax.broadcasted_iota(jnp.int32, (1, atoms), 1)
    targets = lax.broadcasted_iota(jnp.int32, (2 * SUB, atoms), 0)
    total = jnp.zeros((4 * SUB, LANES), jnp.float32)
    places = ((first_row >> 7, first_row & (LANES - 1)), second_place(second_row, width))
    marks = []
    for end, (row, lane) in enumerate(places):
        row = jnp.where(usable, row, -1)
        hits = lane_hits(lane, atoms)
        marks.append((row, hits))
        hit = targets == jnp.broadcast_to(row, targets.shape)
        total = total + nt_dot(split_codes(hit, 2 * node + end + 1), hits)
    sums = 16.0 * total[: 2 * SUB] + total[2 * SUB :]

    valid = (lanes & (HALF - 1)) < width
    slots = jnp.zeros((2 * SUB, LANES), jnp.float32)
    for a in range(3):
        row = jnp.where(valid, ones[a] >> 7, -1)
        hit = sublane == jnp.broadcast_to(row, sublane.shape)
        slots = slots + nt_dot(split_codes(hit, (SUB + a) * LANES + lanes + 1), lane_hits(ones[a] & (LANES - 1), LANES))
    sent_slot = 16.0 * slots[:SUB] + slots[SUB:]
    s_ref[0:SUB, :] = 4096.0 * sums[:SUB] + sent_slot
    out_code = sums[SUB:]

    first = stack_rows(bonds, 0, hold_a)
    second = stack_rows(bonds, 1, hold_b)
    alive = (live[...] != 0) & (first != second)
    me = sublane * LANES + spot
    none = 2 * (2 * atoms - 1)
    table = tile_rows(s_ref)
    ends = ((first >> 7, first & (LANES - 1)), second_place(second, width))
    base = 9 * SUB
    for end, (row, lane) in enumerate(ends):
        both = pick(table, row, lane).astype(jnp.int32)
        code = (both >> 12) - (2 * me + end + 1)
        ghost = both & 4095
        link = jnp.where(code > 0, code - 1, jnp.where(ghost > 0, 2 * (ghost - 1), none))
        if end == 1:
            link = jnp.where(row >= SUB, 2 * (row * LANES + lane), link)
        pub[base + end * SUB : base + (end + 1) * SUB, :] = jnp.where(alive, link, none).astype(jnp.float32)
        lead = jnp.where(alive & (2 * me + end + 1 > code), 1, 0)
        for r in range(SUB):
            row_ref[end : end + 1, r * LANES : (r + 1) * LANES] = lead[r : r + 1]
    sent = pick(table, *sent_place).astype(jnp.int32) >> 12
    in_row = (sublane < 3) & ((spot & (HALF - 1)) < width)
    darts = jnp.where(in_row, sent - 1, jnp.where(sublane >= 4, out_code.astype(jnp.int32) - 1, -1))
    pub[base + 2 * SUB : base + 3 * SUB, :] = darts.astype(jnp.float32)

    total = jnp.zeros((2 * SUB, LANES), jnp.float32)
    for end, (row, hits) in enumerate(marks):
        row = jnp.where(row_ref[end : end + 1, :] != 0, row, -1)
        hit = targets[:SUB] == jnp.broadcast_to(row, (SUB, atoms))
        total = total + nt_dot(split_codes(hit, 2 * node + end + 1), hits)
    lead = 16.0 * total[:SUB] + total[SUB:]
    own[0:SUB, :] = lead.astype(jnp.int32) - 1
    own[SUB : 2 * SUB, :] = (sums[:SUB] - lead).astype(jnp.int32) - 1
    own[2 * SUB : 3 * SUB, :] = sent_slot.astype(jnp.int32) - 1

    tables = [flat_rows(old, q) for q in range(3)] + [flat_rows(new, q) for q in range(3)] + [tile_rows(mass)]
    firsts, seconds = [], []
    for f, table in enumerate(tables):
        firsts.append(pick(table, *ends[0]))
        seconds.append(pick(table, *ends[1]))
        got = pick(table, *sent_place)
        at = FIELDS * SUB + 3 * f
        pub[at : at + 3, :] = got[0:3]
    pub[FIELDS * SUB + 21 : FIELDS * SUB + 24, :] = jnp.zeros((3, LANES), jnp.float32)
    weight = live[...].astype(jnp.float32)
    away = ends[1][0] >= SUB
    span = [weight * (x - y) for x, y in zip(firsts, seconds)]
    scaling = jnp.where(away, 1.0, lax.rsqrt(firsts[6] + seconds[6]))
    norm = jnp.where(away, 1.0, lax.rsqrt(span[0] * span[0] + span[1] * span[1] + span[2] * span[2] + 0.25))
    values = [scaling * norm * span[q] for q in range(3)]
    values = values + [scaling * span[3 + q] for q in range(3)]
    values = values + [scaling * weight * rest[...], firsts[6], seconds[6]]
    for f, value in enumerate(values):
        pub[f * SUB : (f + 1) * SUB, :] = value


def place(dart):
    return dart >> 8, (dart >> 1) & (LANES - 1)


def main_kernel(sizes, ranked, counts, near_list, mass, own, *refs):
    nx, ny, nz = sizes
    pubs = refs[:nx]
    (
        out_disp, out_mult, u_ref, n_ref, rho_ref, mf_ref, mg_ref, p_ref, e_ref,
        eu_ref, g_ref, w_ref, diag_ref, xa, xb, one_ref, two_ref, ep_ref, near,
    ) = refs[nx:]
    here = (lax.axis_index("gy"), lax.axis_index("gz"))
    for at, value in enumerate(near_list):
        near[at] = value
    lower = lax.broadcasted_iota(jnp.int32, (SUB, LANES), 1) < HALF

    def wrap(value, n):
        value = jnp.where(value >= n, value - n, value)
        return jnp.where(value < 0, value + n, value)

    def source(relative):
        dx, dy, dz = (d % n for d, n in zip(relative, sizes))
        return pubs[dx], wrap(here[0] + dy, ny) * nz + wrap(here[1] + dz, nz)

    def load(d):
        pub, s = source(ranked[d])
        field = [pub[s, f * SUB : (f + 1) * SUB, :] for f in range(FIELDS)]
        row, lane = place(field[10].astype(jnp.int32))
        away = (row >= 12) & (row < 15)
        beside = []
        for a in range(3):
            for move in (-1, 1):
                to = list(ranked[d])
                to[a] += move
                beside.append(source(to))
        remote = []
        for f in range(7):
            rows = {}
            for a in range(3):
                at = FIELDS * SUB + 3 * f + a

                def make(a=a, at=at):
                    (down, i), (up, j) = beside[2 * a], beside[2 * a + 1]
                    return jnp.where(lower, wide(down[i, at : at + 1, :]), wide(up[j, at : at + 1, :]))

                rows[12 + a] = make
            remote.append(pick(rows, row, lane))
        span = [field[q] - remote[q] for q in range(6)]
        mf = field[7]
        mg = jnp.where(away, remote[6], field[8])
        both = mf + mg
        scaling = lax.rsqrt(both)
        norm = scaling * lax.rsqrt(span[0] * span[0] + span[1] * span[1] + span[2] * span[2] + 0.25)
        u = [jnp.where(away, norm * span[q], field[q]) for q in range(3)]
        n = [jnp.where(away, scaling * span[3 + q], field[3 + q]) for q in range(3)]
        rho = jnp.where(away, scaling * field[6], field[6])
        root = both * scaling
        size = u[0] * u[0] + u[1] * u[1] + u[2] * u[2]
        dot = u[0] * n[0] + u[1] * n[1] + u[2] * n[2]
        value = dot * root - rho

        def finish():
            diag_ref[d] = 1.0 - both * size
            xa[d] = value
            one_ref[d] = value
            for q in range(3):
                u_ref[d, q] = u[q]
                n_ref[d, q] = n[q]
            rho_ref[d] = rho
            mf_ref[d] = mf
            mg_ref[d] = mg
            p_ref[d, 0] = field[9].astype(jnp.int32)
            p_ref[d, 1] = field[10].astype(jnp.int32)
            e_ref[d] = field[11].astype(jnp.int32)

        return finish

    for c in range(0, len(ranked), LOAD):
        done = [load(d) for d in range(c, min(c + LOAD, len(ranked)))]
        for finish in done:
            finish()

    def chunks(count, body):
        steps = -(-count // CHUNK)

        def step(c, carry):
            done = [body(c * CHUNK + k) for k in range(CHUNK)]
            for finish in done:
                finish()
            return carry

        if steps == 1:
            step(0, 0)
        else:
            lax.fori_loop(0, steps, step, 0)

    def table_of(i, own, ghost):
        rows = {r: functools.partial(own, i, r) for r in range(SUB)}
        for a in range(3):
            down, up = near[6 * i + 2 * a], near[6 * i + 2 * a + 1]

            def into(a=a, down=down, up=up):
                return jnp.where(lower, wide(ghost(up, 4 + a)), wide(ghost(down, 4 + a)))

            def away(a=a, down=down, up=up):
                return jnp.where(lower, wide(ghost(down, a)), wide(ghost(up, a)))

            rows[SUB + a] = into
            rows[SUB + 4 + a] = away
        return rows

    def pick_ends(i, tables):
        loaded = [{number: wide(make()) for number, make in table.items()} for table in tables]
        results = []
        for end in range(2):
            row, lane = place(p_ref[i, end])
            seen = [number for number in loaded[0] if end == 1 or number < SUB + 4]
            hits = {number: row == number for number in seen}
            got = []
            for data in loaded:
                total = jnp.zeros((SUB, LANES), jnp.float32)
                for number in seen:
                    value = jnp.take_along_axis(data[number], lane, axis=1, mode="promise_in_bounds")
                    total = jnp.where(hits[number], value, total)
                got.append(total)
            results.append(got)
        return results

    def pick_two(i, own, ghost):
        one, two = pick_ends(i, [table_of(i, own, ghost)])
        return one[0], two[0]

    def couple_setup(i):
        u = [u_ref[i, q] for q in range(3)]
        mf, mg = mf_ref[i], mg_ref[i]
        signs = [mf * jnp.where((p_ref[i, 0] & 1) == 1, -1.0, 1.0), -mg * jnp.where((p_ref[i, 1] & 1) == 1, -1.0, 1.0)]
        weights = [jnp.zeros((SUB, LANES), jnp.float32)] * 2
        pulls = []
        tables = [
            table_of(i, lambda i, r, q=q: u_ref[i, q, r : r + 1, :], lambda i, r, q=q: eu_ref[i, q, r : r + 1, :])
            for q in range(3)
        ]
        for end, got in enumerate(pick_ends(i, tables)):
            for q in range(3):
                pull = signs[end] * got[q]
                weights[end] = weights[end] + u[q] * pull
                pulls.append((end * 3 + q, pull))

        def finish():
            for at, pull in pulls:
                g_ref[i, at] = pull
            for end in range(2):
                w_ref[i, end] = weights[end]

        return finish

    def unit_ends(i):
        dart = e_ref[i]
        row, lane = place(dart)
        sign = jnp.where((dart & 1) == 1, -1.0, 1.0)
        ends = [
            sign * pick({r: functools.partial(lambda q, r: u_ref[i, q, r : r + 1, :], q, r) for r in range(SUB)}, row, lane)
            for q in range(3)
        ]

        def finish():
            for q in range(3):
                eu_ref[i, q] = ends[q]

        return finish

    chunks(counts[REACH], unit_ends)
    chunks(counts[REACH - 1], couple_setup)

    def send_ends(x, count):
        def body(i):
            row, lane = place(e_ref[i])
            got = pick({r: functools.partial(lambda r: x[i, r : r + 1, :], r) for r in range(SUB)}, row, lane)

            def finish():
                ep_ref[i] = got

            return finish

        chunks(count, body)

    def own_of(x):
        return lambda i, r: x[i, r : r + 1, :]

    def ghost_value(i, r):
        return ep_ref[i, r : r + 1, :]

    def expand(current, following, total, reach):
        for term in range(ORDER):
            send_ends(current, counts[reach - term])

            def body(i, current=current, following=following):
                got = pick_two(i, own_of(current), ghost_value)
                value = diag_ref[i] * current[i] - w_ref[i, 0] * got[0] - w_ref[i, 1] * got[1]

                def finish():
                    following[i] = value
                    total[i] = total[i] + value

                return finish

            chunks(counts[reach - term - 1], body)
            current, following = following, current

    expand(xa, xb, one_ref, REACH)
    send_ends(one_ref, counts[ORDER + 2])

    def correct(i):
        got = pick_two(i, own_of(one_ref), ghost_value)
        both = mf_ref[i] + mg_ref[i]
        scaling = lax.rsqrt(both)
        mine = both * one_ref[i]
        length = jnp.zeros((SUB, LANES), jnp.float32)
        for q in range(3):
            part = n_ref[i, q] - scaling * (u_ref[i, q] * mine + g_ref[i, q] * got[0] + g_ref[i, 3 + q] * got[1])
            length = length + part * part
        rho = rho_ref[i]
        square = rho * rho
        value = rho - jnp.sqrt(jnp.maximum(2.0 * square - length, 0.25 * square))

        def finish():
            xa[i] = value
            two_ref[i] = value

        return finish

    chunks(counts[ORDER + 1], correct)
    expand(xa, xb, two_ref, ORDER + 1)

    def join(i):
        value = one_ref[i] + two_ref[i]

        def finish():
            xa[i] = value

        return finish

    chunks(counts[1], join)
    send_ends(xa, counts[1])

    multiplier = xa[0]
    out_mult[...] = multiplier
    for q in range(3):
        xb[q] = u_ref[0, q] * multiplier
    narrow = lower[0:1]
    total = [jnp.zeros((SUB, LANES), jnp.float32)] * 3
    for end in range(2):
        dart = own[end * SUB : (end + 1) * SUB, :]
        row, lane = place(dart)
        sign = jnp.where((dart & 1) == 1, -1.0, 1.0)
        for q in range(3):
            rows = {r: functools.partial(lambda q, r: xb[q, r : r + 1, :], q, r) for r in range(SUB)}
            total[q] = total[q] + sign * pick(rows, row, lane)
    ghost = own[2 * SUB : 3 * SUB, :]
    for q in range(3):
        rows = {}
        for a in range(3):

            def make(a=a, q=q):
                down, up = near_list[2 * a], near_list[2 * a + 1]
                at = 4 + a
                from_up = eu_ref[up, q, at : at + 1, :] * ep_ref[up, at : at + 1, :]
                from_down = eu_ref[down, q, at : at + 1, :] * ep_ref[down, at : at + 1, :]
                return jnp.where(narrow, from_up, from_down)

            rows[SUB + a] = make
        value = -mass[...] * (total[q] + pick(rows, ghost >> 7, ghost & (LANES - 1)))
        for r in range(SUB):
            out_disp[q : q + 1, r * LANES : (r + 1) * LANES] = value[r : r + 1]


def domains_near(sizes):
    def far(d, n):
        return min(d, n - d)

    ranked = sorted(
        itertools.product(*(range(n) for n in sizes)), key=lambda r: (sum(far(d, n) for d, n in zip(r, sizes)), r)
    )
    span = [sum(far(d, n) for d, n in zip(r, sizes)) for r in ranked]
    ranked = [r for r, s in zip(ranked, span) if s <= REACH]
    counts = [sum(s <= d for s in span) for d in range(REACH + 1)]
    at = {r: i for i, r in enumerate(ranked)}
    near = []
    for r in ranked:
        for a in range(3):
            for move in (-1, 1):
                to = list(r)
                to[a] = (to[a] + move) % sizes[a]
                near.append(at.get(tuple(to), 0))
    return ranked, counts, near


def per_device(old_pos, new_pos, inv_mass, rest_length, bond_pairs, live, send_index):
    sizes = [lax.axis_size(axis) for axis in AXES]
    nx, ny, nz = sizes
    atoms = old_pos.shape[1]
    width = send_index.shape[1]
    tile = (SUB, LANES)
    mass, rest, alive = (v.reshape(tile) for v in (inv_mass, rest_length, live))
    f32, i32 = jnp.float32, jnp.int32
    shape = jax.ShapeDtypeStruct

    pub, own = pl.pallas_call(
        functools.partial(publish_kernel, width),
        out_shape=[shape((FIELDS * SUB + 24, LANES), f32), shape((3 * SUB, LANES), i32)],
        in_specs=[VMEM] * 8,
        out_specs=[VMEM] * 2,
        scratch_shapes=[pltpu.VMEM(tile, i32)] * 3 + [pltpu.VMEM(tile, f32), pltpu.VMEM((2, atoms), i32)],
        name="publish",
    )(old_pos, new_pos, mass, rest, alive, live.reshape(1, atoms), bond_pairs, send_index)

    plane = ny * nz
    gathered = lax.all_to_all(jnp.broadcast_to(pub, (plane,) + pub.shape), ("gy", "gz"), 0, 0)
    parts = [gathered]
    for d in range(1, nx):
        parts.append(lax.ppermute(gathered, "gx", [(i, (i - d) % nx) for i in range(nx)]))

    ranked, counts, near = domains_near(sizes)
    held = -(-len(ranked) // CHUNK) * CHUNK
    near = near + [0] * (6 * (held - len(ranked)))

    def keep(*lead, kind=f32):
        return pltpu.VMEM(lead + tile, kind)

    disp, mult = pl.pallas_call(
        functools.partial(main_kernel, sizes, ranked, counts, near),
        out_shape=[shape((3, atoms), f32), shape(tile, f32)],
        in_specs=[VMEM] * (2 + nx),
        out_specs=[VMEM] * 2,
        scratch_shapes=[
            keep(held, 3), keep(held, 3), keep(held), keep(held), keep(held), keep(held, 2, kind=i32), keep(held, kind=i32),
            keep(held, 3), keep(held, 6), keep(held, 2), keep(held), keep(held), keep(held), keep(held), keep(held), keep(held),
            pltpu.SMEM((len(near),), i32),
        ],
        name="solve",
    )(mass, own, *parts)
    return disp, mult.reshape(atoms)


def solution(mesh):
    flat = P(AXES)
    rows = P(None, AXES)
    return jax.shard_map(
        per_device,
        mesh=mesh,
        in_specs=(rows, rows, flat, flat, rows, flat, P(AXES, None)),
        out_specs=(rows, flat),
        check_vma=False,
    )
```

time: 68.8 us -> 62.3 us (0.906)
  blocking collectives: 23 us -> 33.3 us
  starting transfers between devices: 7.6 us -> 0.01 us
  Pallas kernels: 28 us -> 23.6 us
  waiting for transfers between devices: 5.38 us -> 2.56 us
  local copies, waits for them, and re-layouts: 3.1 us -> 1.89 us
    all_to_all x1, blocking collectives: 23 us -> 33.3 us  [per_device(): lax.all_to_all(jnp.broadcast_to(pub, (plane,) + pub.shape), ('gy', 'gz'),...]
    ppermute x4 -> x0, starting transfers between devices: 7.6 us -> none  [the longest x1 4.56 us: per_device(): lax.ppermute(part, axis, [(i, (i - 1) % n) for i in range(n)])]
    ppermute x4 -> x0, waiting for transfers between devices: 4.42 us -> none  [the longest x3 4.41 us: per_device(): low = lax.ppermute(part, axis, [(i, (i + 1) % n) for i in range(n)])]
    pallas_call x4 -> x2, Pallas kernels: 28 us -> 23.6 us  [the longest x1 21.4 us: per_device(): pl.pallas_call(functools.partial(main_kernel, sizes, ranked, counts, near...]
    ppermute x1, waiting for transfers between devices: 0.97 us -> 2.56 us  [per_device(): lax.ppermute(gathered, 'gx', [(i, (i - d) % nx) for i in range(nx)])]
    unnamed x18 -> x4, local copies, waits for them, and re-layouts: 2.24 us -> 0.99 us
  transfers between devices with their start and end apart: 5 -> 1, of which waited for: 2 -> 1; matrix products, arithmetic and copies ran while one was open for 1% -> 0% of each run, Pallas kernels for 3% -> 0%
where the time goes in v2:
time: 62.3 us; the launch traced here: 62 us
  blocking collectives  33.3 us (53%)
  Pallas kernels  23.6 us (38%)
  waiting for transfers between devices  2.56 us (4%)
  local copies, waits for them, and re-layouts  1.89 us (3%)
  between operations  0.64 us (1%)
    all_to_all x1, blocking collectives, per_device(): lax.all_to_all(jnp.broadcast_to(pub, (plane,) + pub.shape), ('gy', 'gz'),...  33.3 us
    pallas_call x1, Pallas kernels, per_device(): pl.pallas_call(functools.partial(main_kernel, sizes, ranked, counts, near...  21.4 us
    ppermute x1, waiting for transfers between devices, per_device(): lax.ppermute(gathered, 'gx', [(i, (i - d) % nx) for i in range(nx)])  2.56 us
    pallas_call x1, Pallas kernels, per_device(): pl.pallas_call(functools.partial(publish_kernel, width), out_shape=[shape...  2.22 us
  transfers between devices with their start and end apart: 1, of which 1 were waited for; matrix products, arithmetic and copies ran while one was open for 0% of the time, Pallas kernels for 0%

profile of v2, /device:TPU:0, one launch (start us, length us, event | category | flops | bytes accessed | tf_op | source)
XLA Modules:
  0.0 62.0 jit_solution(8403392225518982898)
XLA Ops:
  0.6 2.2 %publish.1 = (f32[120,128]{1,0:T(8,128)}, s32[24,128]{1,0:T(8,128)}) custom-call(f32[3,1024]{1,0:T(4,128)} %old.1, f32[3,1024]{1,0:T(4,128)} %new.1, f32[8,128]{1,0:T(8,128)} %bitcast.5, f32[8,128]{1,0:T(8,128)} %bitcast.9, s32[8,128]{1,0:T(8,128)} %bitcast.7, s32[1,1024]{1,0:T(1,128)} %bitcast.8, s32[2,1024]{1,0:T(2,128)} %bonds.1, s32[6,48]{1,0:T(8,128)} %send.1), custom_call_target="tpu_custom_call" | custom-call | tf_op jit(solution)/shard_map/publish/pallas_call | solution.py:483
  2.8 0.9 %broadcast_in_dim.3 = f32[16,120,128]{2,1,0:T(8,128)S(1)} broadcast(f32[120,128]{1,0:T(8,128)} %get-tuple-element.7), dimensions={1,2} | broadcast | bytes 1044480 | tf_op jit(solution)/shard_map/broadcast_in_dim | solution.py:493
  3.7 33.3 %all_to_all.5.refs_0_ = f32[16,120,128]{2,1,0:T(8,128)S(1)} all-to-all(f32[16,120,128]{2,1,0:T(8,128)S(1)} %broadcast_in_dim.3), channel_id=1, replica_groups=mesh['gx'=2,'gy'=2,'gz'=8] {'gy','gz'}, dimensions={0} | all-to-all | bytes 1966080 | tf_op jit(solution)/shard_map/all_to_all | solution.py:493
  37.0 0.0 copy-start
  37.0 0.0 collective-permute-start
  37.0 2.6 %collective-permute-done.refs_1_ = f32[16,120,128]{2,1,0:T(8,128)S(1)} collective-permute-done((f32[16,120,128]{2,1,0:T(8,128)S(1)}, f32[16,120,128]{2,1,0:T(8,128)S(1)}, u32[]{:S(2)}, u32[]{:S(2)}) %collective-permute-start) | collective-permute-done | bytes 983072 | tf_op jit(solution)/shard_map/ppermute | solution.py:496
  39.6 0.0 copy-start.1
  39.6 0.0 copy-done
  39.6 1.0 %copy-done.1 = f32[16,120,128]{2,1,0:T(8,128)} copy-done((f32[16,120,128]{2,1,0:T(8,128)}, f32[16,120,128]{2,1,0:T(8,128)S(1)}, u32[]{:S(2)}) %copy-start.1) | copy-done | bytes 983064
  40.6 21.4 %solve.1 = (f32[3,1024]{1,0:T(4,128)}, f32[8,128]{1,0:T(8,128)}) custom-call(f32[8,128]{1,0:T(8,128)} %bitcast.6, s32[24,128]{1,0:T(8,128)} %get-tuple-element.6.own, f32[16,120,128]{2,1,0:T(8,128)} %copy-done, f32[16,120,128]{2,1,0:T(8,128)} %copy-done.1), custom_call_target="tpu_custom_call" | custom-call | tf_op jit(solution)/shard_map/solve/pallas_call | solution.py:505
Async XLA Ops:
  37.0 2.6 %copy-start = (f32[16,120,128]{2,1,0:T(8,128)}, f32[16,120,128]{2,1,0:T(8,128)S(1)}, u32[]{:S(2)}) copy-start(f32[16,120,128]{2,1,0:T(8,128)S(1)} %all_to_all.5.refs_0_) | copy-start | bytes 2949124
  37.0 2.6 %collective-permute-start = (f32[16,120,128]{2,1,0:T(8,128)S(1)}, f32[16,120,128]{2,1,0:T(8,128)S(1)}, u32[]{:S(2)}, u32[]{:S(2)}) collective-permute-start(f32[16,120,128]{2,1,0:T(8,128)S(1)} %all_to_all.5.refs_0_), channel_id=1, source_target_pairs={{0,16},{16,0},{1,17},{17,1},{2,18},{18,2},{3,19},{19,3},{4,20},{20... | collective-permute-start | bytes 2949128 | tf_op jit(solution)/shard_map/ppermute | solution.py:496
  39.6 1.0 %copy-start.1 = (f32[16,120,128]{2,1,0:T(8,128)}, f32[16,120,128]{2,1,0:T(8,128)S(1)}, u32[]{:S(2)}) copy-start(f32[16,120,128]{2,1,0:T(8,128)S(1)} %collective-permute-done.refs_1_) | copy-start | bytes 2949124

commit v3 on v2

--- a/solution.py
+++ b/solution.py
@@ -16,7 +16,7 @@
 SUB = 8
 CHUNK = 16
 LOAD = 4
-FIELDS = 12
+FIELDS = 11
 REACH = 2 * (ORDER + 1)
 VMEM = pl.BlockSpec(memory_space=pltpu.VMEM)
 
@@ -140,7 +140,10 @@
     sent = pick(table, *sent_place).astype(jnp.int32) >> 12
     in_row = (sublane < 3) & ((spot & (HALF - 1)) < width)
     darts = jnp.where(in_row, sent - 1, jnp.where(sublane >= 4, out_code.astype(jnp.int32) - 1, -1))
-    pub[base + 2 * SUB : base + 3 * SUB, :] = darts.astype(jnp.float32)
+    tail = FIELDS * SUB
+    darts = darts.astype(jnp.float32)
+    pub[tail : tail + 3, :] = darts[0:3]
+    pub[tail + 3 : tail + 6, :] = darts[4:7]
 
     total = jnp.zeros((2 * SUB, LANES), jnp.float32)
     for end, (row, hits) in enumerate(marks):
@@ -153,14 +156,13 @@
     own[2 * SUB : 3 * SUB, :] = sent_slot.astype(jnp.int32) - 1
 
     tables = [flat_rows(old, q) for q in range(3)] + [flat_rows(new, q) for q in range(3)] + [tile_rows(mass)]
-    firsts, seconds = [], []
-    for f, table in enumerate(tables):
-        firsts.append(pick(table, *ends[0]))
-        seconds.append(pick(table, *ends[1]))
-        got = pick(table, *sent_place)
-        at = FIELDS * SUB + 3 * f
-        pub[at : at + 3, :] = got[0:3]
-    pub[FIELDS * SUB + 21 : FIELDS * SUB + 24, :] = jnp.zeros((3, LANES), jnp.float32)
+    firsts = [pick(table, *ends[0]) for table in tables]
+    seconds = [pick(table, *ends[1]) for table in tables]
+    heavy = pick(tables[6], *sent_place)
+    for f in range(6):
+        moved = pltpu.roll(heavy, (width - f * (HALF - width)) % LANES, 1)
+        got = jnp.where((spot & (HALF - 1)) < width, pick(tables[f], *sent_place), moved)
+        pub[tail + 6 + 3 * f : tail + 9 + 3 * f, :] = got[0:3]
     weight = live[...].astype(jnp.float32)
     away = ends[1][0] >= SUB
     span = [weight * (x - y) for x, y in zip(firsts, seconds)]
@@ -177,12 +179,12 @@
     return dart >> 8, (dart >> 1) & (LANES - 1)
 
 
-def main_kernel(sizes, ranked, counts, near_list, mass, own, *refs):
+def main_kernel(sizes, width, ranked, counts, near_list, mass, own, *refs):
     nx, ny, nz = sizes
     pubs = refs[:nx]
     (
         out_disp, out_mult, u_ref, n_ref, rho_ref, mf_ref, mg_ref, p_ref, e_ref,
-        eu_ref, g_ref, w_ref, diag_ref, xa, xb, one_ref, two_ref, ep_ref, near,
+        eu_ref, g_ref, w_ref, diag_ref, xa, xb, one_ref, two_ref, ea, eb, near,
     ) = refs[nx:]
     here = (lax.axis_index("gy"), lax.axis_index("gz"))
     for at, value in enumerate(near_list):
@@ -196,6 +198,10 @@
     def source(relative):
         dx, dy, dz = (d % n for d, n in zip(relative, sizes))
         return pubs[dx], wrap(here[0] + dy, ny) * nz + wrap(here[1] + dz, nz)
+
+    def ends_of(value, dart):
+        row, lane = place(dart)
+        return pick({r: functools.partial(lambda r: value(r), r) for r in range(SUB)}, row, lane)
 
     def load(d):
         pub, s = source(ranked[d])
@@ -208,18 +214,18 @@
                 to = list(ranked[d])
                 to[a] += move
                 beside.append(source(to))
-        remote = []
-        for f in range(7):
-            rows = {}
-            for a in range(3):
-                at = FIELDS * SUB + 3 * f + a
-
-                def make(a=a, at=at):
-                    (down, i), (up, j) = beside[2 * a], beside[2 * a + 1]
-                    return jnp.where(lower, wide(down[i, at : at + 1, :]), wide(up[j, at : at + 1, :]))
-
-                rows[12 + a] = make
-            remote.append(pick(rows, row, lane))
+        def sent_row(f, a):
+            at = FIELDS * SUB + 6 + 3 * f + a
+            (down, i), (up, j) = beside[2 * a], beside[2 * a + 1]
+            return jnp.where(lower, wide(down[i, at : at + 1, :]), wide(up[j, at : at + 1, :]))
+
+        sent = {(f, a): sent_row(f, a) for f in range(6) for a in range(3)}
+        remote = [pick({12 + a: functools.partial(sent.get, (f, a)) for a in range(3)}, row, lane) for f in range(6)]
+        spare = HALF - width
+        inner = lane & (HALF - 1)
+        piece = sum((inner >= f * spare).astype(jnp.int32) for f in range(1, -(-width // spare)))
+        tables = {16 * f + 12 + a: functools.partial(sent.get, (f, a)) for f in range(-(-width // spare)) for a in range(3)}
+        remote.append(pick(tables, 16 * piece + row, (lane - inner) + width + inner - piece * spare))
         span = [field[q] - remote[q] for q in range(6)]
         mf = field[7]
         mg = jnp.where(away, remote[6], field[8])
@@ -233,6 +239,8 @@
         size = u[0] * u[0] + u[1] * u[1] + u[2] * u[2]
         dot = u[0] * n[0] + u[1] * n[1] + u[2] * n[2]
         value = dot * root - rho
+        at = FIELDS * SUB
+        darts = [pub[s, at + 3 * h : at + 3 * h + 3, :].astype(jnp.int32) for h in range(2)]
 
         def finish():
             diag_ref[d] = 1.0 - both * size
@@ -246,22 +254,48 @@
             mg_ref[d] = mg
             p_ref[d, 0] = field[9].astype(jnp.int32)
             p_ref[d, 1] = field[10].astype(jnp.int32)
-            e_ref[d] = field[11].astype(jnp.int32)
+            e_ref[d] = jnp.full((SUB, LANES), -1, jnp.int32)
+            e_ref[d, 0:3] = darts[0]
+            e_ref[d, 4:7] = darts[1]
 
         return finish
 
+    def load_ends(d):
+        dart = e_ref[d]
+        sign = jnp.where((dart & 1) == 1, -1.0, 1.0)
+        unit = [sign * ends_of(lambda r, q=q: u_ref[d, q, r : r + 1, :], dart) for q in range(3)]
+        ends = ends_of(lambda r: xa[d, r : r + 1, :], dart)
+
+        def finish():
+            ea[d] = ends
+            for q in range(3):
+                eu_ref[d, q] = unit[q]
+
+        return finish
+
     for c in range(0, len(ranked), LOAD):
-        done = [load(d) for d in range(c, min(c + LOAD, len(ranked)))]
-        for finish in done:
+        group = range(c, min(c + LOAD, len(ranked)))
+        for finish in [load(d) for d in group]:
             finish()
-
-    def chunks(count, body):
+        for finish in [load_ends(d) for d in group]:
+            finish()
+
+    def chunks(count, body, x, ep):
         steps = -(-count // CHUNK)
+        size = -(-count // steps)
+
+        def ends(i):
+            got = ends_of(lambda r: x[i, r : r + 1, :], e_ref[i])
+
+            def finish():
+                ep[i] = got
+
+            return finish
 
         def step(c, carry):
-            done = [body(c * CHUNK + k) for k in range(CHUNK)]
-            for finish in done:
-                finish()
+            for part in (body, ends):
+                for finish in [part(c * size + k) for k in range(size)]:
+                    finish()
             return carry
 
         if steps == 1:
@@ -305,91 +339,73 @@
         one, two = pick_ends(i, [table_of(i, own, ghost)])
         return one[0], two[0]
 
-    def couple_setup(i):
+    def couple(i):
         u = [u_ref[i, q] for q in range(3)]
         mf, mg = mf_ref[i], mg_ref[i]
         signs = [mf * jnp.where((p_ref[i, 0] & 1) == 1, -1.0, 1.0), -mg * jnp.where((p_ref[i, 1] & 1) == 1, -1.0, 1.0)]
-        weights = [jnp.zeros((SUB, LANES), jnp.float32)] * 2
-        pulls = []
         tables = [
             table_of(i, lambda i, r, q=q: u_ref[i, q, r : r + 1, :], lambda i, r, q=q: eu_ref[i, q, r : r + 1, :])
             for q in range(3)
         ]
+        tables.append(table_of(i, lambda i, r: xa[i, r : r + 1, :], lambda i, r: ea[i, r : r + 1, :]))
+        value = diag_ref[i] * xa[i]
+        pulls, weights = [], []
         for end, got in enumerate(pick_ends(i, tables)):
-            for q in range(3):
-                pull = signs[end] * got[q]
-                weights[end] = weights[end] + u[q] * pull
-                pulls.append((end * 3 + q, pull))
+            pull = [signs[end] * got[q] for q in range(3)]
+            weight = u[0] * pull[0] + u[1] * pull[1] + u[2] * pull[2]
+            value = value - weight * got[3]
+            pulls = pulls + pull
+            weights.append(weight)
+        added = one_ref[i] + value
 
         def finish():
-            for at, pull in pulls:
+            for at, pull in enumerate(pulls):
                 g_ref[i, at] = pull
             for end in range(2):
                 w_ref[i, end] = weights[end]
+            xb[i] = value
+            one_ref[i] = added
 
         return finish
 
-    def unit_ends(i):
-        dart = e_ref[i]
-        row, lane = place(dart)
-        sign = jnp.where((dart & 1) == 1, -1.0, 1.0)
-        ends = [
-            sign * pick({r: functools.partial(lambda q, r: u_ref[i, q, r : r + 1, :], q, r) for r in range(SUB)}, row, lane)
-            for q in range(3)
-        ]
-
-        def finish():
-            for q in range(3):
-                eu_ref[i, q] = ends[q]
-
-        return finish
-
-    chunks(counts[REACH], unit_ends)
-    chunks(counts[REACH - 1], couple_setup)
-
-    def send_ends(x, count):
-        def body(i):
-            row, lane = place(e_ref[i])
-            got = pick({r: functools.partial(lambda r: x[i, r : r + 1, :], r) for r in range(SUB)}, row, lane)
-
-            def finish():
-                ep_ref[i] = got
-
-            return finish
-
-        chunks(count, body)
+    chunks(counts[REACH - 1], couple, xb, eb)
+
+    def ghost_of(ep):
+        return lambda i, r: ep[i, r : r + 1, :]
 
     def own_of(x):
         return lambda i, r: x[i, r : r + 1, :]
 
-    def ghost_value(i, r):
-        return ep_ref[i, r : r + 1, :]
-
-    def expand(current, following, total, reach):
-        for term in range(ORDER):
-            send_ends(current, counts[reach - term])
-
-            def body(i, current=current, following=following):
-                got = pick_two(i, own_of(current), ghost_value)
+    def expand(state, total, reach, first, closing):
+        for term in range(first, ORDER):
+            (current, ep), (following, ep_next) = state
+            last = term == ORDER - 1
+
+            def body(i, current=current, ep=ep, following=following, ep_next=ep_next, last=last):
+                got = pick_two(i, own_of(current), ghost_of(ep))
                 value = diag_ref[i] * current[i] - w_ref[i, 0] * got[0] - w_ref[i, 1] * got[1]
+                added = total[i] + value
+                if last:
+                    value = closing(i, added)
 
                 def finish():
+                    total[i] = added
                     following[i] = value
-                    total[i] = total[i] + value
 
                 return finish
 
-            chunks(counts[reach - term - 1], body)
-            current, following = following, current
-
-    expand(xa, xb, one_ref, REACH)
-    send_ends(one_ref, counts[ORDER + 2])
+            chunks(counts[reach - term - 1], body, following, ep_next)
+            state = state[::-1]
+        return state
+
+    state = expand(((xb, eb), (xa, ea)), one_ref, REACH, 1, lambda i, added: added)
 
     def correct(i):
-        got = pick_two(i, own_of(one_ref), ghost_value)
+        (current, ep), _ = state
+        got = pick_two(i, own_of(current), ghost_of(ep))
         both = mf_ref[i] + mg_ref[i]
         scaling = lax.rsqrt(both)
-        mine = both * one_ref[i]
+        mine = both * current[i]
         length = jnp.zeros((SUB, LANES), jnp.float32)
         for q in range(3):
             part = n_ref[i, q] - scaling * (u_ref[i, q] * mine + g_ref[i, q] * got[0] + g_ref[i, 3 + q] * got[1])
@@ -399,29 +415,19 @@
         value = rho - jnp.sqrt(jnp.maximum(2.0 * square - length, 0.25 * square))
 
         def finish():
-            xa[i] = value
+            state[1][0][i] = value
             two_ref[i] = value
 
         return finish
 
-    chunks(counts[ORDER + 1], correct)
-    expand(xa, xb, two_ref, ORDER + 1)
-
-    def join(i):
-        value = one_ref[i] + two_ref[i]
-
-        def finish():
-            xa[i] = value
-
-        return finish
-
-    chunks(counts[1], join)
-    send_ends(xa, counts[1])
-
-    multiplier = xa[0]
+    chunks(counts[ORDER + 1], correct, *state[1])
+    state = expand(state[::-1], two_ref, ORDER + 1, 0, lambda i, added: one_ref[i] + added)
+    (joint, ep_ref), (spare, _) = state
+
+    multiplier = joint[0]
     out_mult[...] = multiplier
     for q in range(3):
-        xb[q] = u_ref[0, q] * multiplier
+        spare[q] = u_ref[0, q] * multiplier
     narrow = lower[0:1]
     total = [jnp.zeros((SUB, LANES), jnp.float32)] * 3
     for end in range(2):
@@ -429,7 +435,7 @@
         row, lane = place(dart)
         sign = jnp.where((dart & 1) == 1, -1.0, 1.0)
         for q in range(3):
-            rows = {r: functools.partial(lambda q, r: xb[q, r : r + 1, :], q, r) for r in range(SUB)}
+            rows = {r: functools.partial(lambda q, r: spare[q, r : r + 1, :], q, r) for r in range(SUB)}
             total[q] = total[q] + sign * pick(rows, row, lane)
     ghost = own[2 * SUB : 3 * SUB, :]
     for q in range(3):
@@ -496,20 +502,20 @@
         parts.append(lax.ppermute(gathered, "gx", [(i, (i - d) % nx) for i in range(nx)]))
 
     ranked, counts, near = domains_near(sizes)
-    held = -(-len(ranked) // CHUNK) * CHUNK
+    held = len(ranked) + CHUNK
     near = near + [0] * (6 * (held - len(ranked)))
 
     def keep(*lead, kind=f32):
         return pltpu.VMEM(lead + tile, kind)
 
     disp, mult = pl.pallas_call(
-        functools.partial(main_kernel, sizes, ranked, counts, near),
+        functools.partial(main_kernel, sizes, width, ranked, counts, near),
         out_shape=[shape((3, atoms), f32), shape(tile, f32)],
         in_specs=[VMEM] * (2 + nx),
         out_specs=[VMEM] * 2,
         scratch_shapes=[
             keep(held, 3), keep(held, 3), keep(held), keep(held), keep(held), keep(held, 2, kind=i32), keep(held, kind=i32),
-            keep(held, 3), keep(held, 6), keep(held, 2), keep(held), keep(held), keep(held), keep(held), keep(held), keep(held),
+            keep(held, 3), keep(held, 6), keep(held, 2), keep(held), keep(held), keep(held), keep(held), keep(held), keep(held), keep(held),
             pltpu.SMEM((len(near),), i32),
         ],
         name="solve",

time: 62.3 us -> 58 us (0.931)
  Pallas kernels: 23.6 us -> 20.8 us
  blocking collectives: 33.3 us -> 32 us
    pallas_call x1, Pallas kernels: 21.4 us -> 18.5 us  [per_device(): pl.pallas_call(functools.partial(main_kernel, sizes, width, ranked, count...]
    all_to_all x1, blocking collectives: 33.3 us -> 32 us  [per_device(): lax.all_to_all(jnp.broadcast_to(pub, (plane,) + pub.shape), ('gy', 'gz'),...]
where the time goes in v3:
time: 58 us; the launch traced here: 57.7 us
  blocking collectives  32 us (55%)
  Pallas kernels  20.8 us (36%)
  waiting for transfers between devices  2.47 us (4%)
  local copies, waits for them, and re-layouts  1.84 us (3%)
  between operations  0.64 us (1%)
    all_to_all x1, blocking collectives, per_device(): lax.all_to_all(jnp.broadcast_to(pub, (plane,) + pub.shape), ('gy', 'gz'),...  32 us
    pallas_call x1, Pallas kernels, per_device(): pl.pallas_call(functools.partial(main_kernel, sizes, width, ranked, count...  18.5 us
    ppermute x1, waiting for transfers between devices, per_device(): lax.ppermute(gathered, 'gx', [(i, (i - d) % nx) for i in range(nx)])  2.47 us
    pallas_call x1, Pallas kernels, per_device(): pl.pallas_call(functools.partial(publish_kernel, width), out_shape=[shape...  2.22 us
  transfers between devices with their start and end apart: 1, of which 1 were waited for; matrix products, arithmetic and copies ran while one was open for 0% of the time, Pallas kernels for 0%

profile of v3, /device:TPU:0, one launch (start us, length us, event | category | flops | bytes accessed | tf_op | source)
XLA Modules:
  0.0 57.7 jit_solution(16618057555872086636)
XLA Ops:
  0.6 2.2 %publish.1 = (f32[112,128]{1,0:T(8,128)}, s32[24,128]{1,0:T(8,128)}) custom-call(f32[3,1024]{1,0:T(4,128)} %old.1, f32[3,1024]{1,0:T(4,128)} %new.1, f32[8,128]{1,0:T(8,128)} %bitcast.5, f32[8,128]{1,0:T(8,128)} %bitcast.9, s32[8,128]{1,0:T(8,128)} %bitcast.7, s32[1,1024]{1,0:T(1,128)} %bitcast.8, s32[2,1024]{1,0:T(2,128)} %bonds.1, s32[6,48]{1,0:T(8,128)} %send.1), custom_call_target="tpu_custom_call" | custom-call | tf_op jit(solution)/shard_map/publish/pallas_call | solution.py:489
  2.9 0.9 %broadcast_in_dim.3 = f32[16,112,128]{2,1,0:T(8,128)S(1)} broadcast(f32[112,128]{1,0:T(8,128)} %get-tuple-element.7), dimensions={1,2} | broadcast | bytes 974848 | tf_op jit(solution)/shard_map/broadcast_in_dim | solution.py:499
  3.7 32.0 %all_to_all.5.refs_0_ = f32[16,112,128]{2,1,0:T(8,128)S(1)} all-to-all(f32[16,112,128]{2,1,0:T(8,128)S(1)} %broadcast_in_dim.3), channel_id=1, replica_groups=mesh['gx'=2,'gy'=2,'gz'=8] {'gy','gz'}, dimensions={0} | all-to-all | bytes 1835008 | tf_op jit(solution)/shard_map/all_to_all | solution.py:499
  35.7 0.0 copy-start
  35.7 0.0 collective-permute-start
  35.7 2.5 %collective-permute-done.refs_1_ = f32[16,112,128]{2,1,0:T(8,128)S(1)} collective-permute-done((f32[16,112,128]{2,1,0:T(8,128)S(1)}, f32[16,112,128]{2,1,0:T(8,128)S(1)}, u32[]{:S(2)}, u32[]{:S(2)}) %collective-permute-start) | collective-permute-done | bytes 917536 | tf_op jit(solution)/shard_map/ppermute | solution.py:502
  38.2 0.0 copy-start.1
  38.2 0.0 copy-done
  38.2 1.0 %copy-done.1 = f32[16,112,128]{2,1,0:T(8,128)} copy-done((f32[16,112,128]{2,1,0:T(8,128)}, f32[16,112,128]{2,1,0:T(8,128)S(1)}, u32[]{:S(2)}) %copy-start.1) | copy-done | bytes 917528
  39.1 18.5 %solve.1 = (f32[3,1024]{1,0:T(4,128)}, f32[8,128]{1,0:T(8,128)}) custom-call(f32[8,128]{1,0:T(8,128)} %bitcast.6, s32[24,128]{1,0:T(8,128)} %get-tuple-element.6.own, f32[16,112,128]{2,1,0:T(8,128)} %copy-done, f32[16,112,128]{2,1,0:T(8,128)} %copy-done.1), custom_call_target="tpu_custom_call" | custom-call | tf_op jit(solution)/shard_map/solve/pallas_call | solution.py:511
Async XLA Ops:
  35.7 2.5 %copy-start = (f32[16,112,128]{2,1,0:T(8,128)}, f32[16,112,128]{2,1,0:T(8,128)S(1)}, u32[]{:S(2)}) copy-start(f32[16,112,128]{2,1,0:T(8,128)S(1)} %all_to_all.5.refs_0_) | copy-start | bytes 2752516
  35.7 2.5 %collective-permute-start = (f32[16,112,128]{2,1,0:T(8,128)S(1)}, f32[16,112,128]{2,1,0:T(8,128)S(1)}, u32[]{:S(2)}, u32[]{:S(2)}) collective-permute-start(f32[16,112,128]{2,1,0:T(8,128)S(1)} %all_to_all.5.refs_0_), channel_id=1, source_target_pairs={{0,16},{16,0},{1,17},{17,1},{2,18},{18,2},{3,19},{19,3},{4,20},{20... | collective-permute-start | bytes 2752520 | tf_op jit(solution)/shard_map/ppermute | solution.py:502
  38.2 1.0 %copy-start.1 = (f32[16,112,128]{2,1,0:T(8,128)}, f32[16,112,128]{2,1,0:T(8,128)S(1)}, u32[]{:S(2)}) copy-start(f32[16,112,128]{2,1,0:T(8,128)S(1)} %collective-permute-done.refs_1_) | copy-start | bytes 2752516

commit v4 on v3

--- a/solution.py
+++ b/solution.py
@@ -75,7 +75,18 @@
     return jnp.where(hits, 1.0, 0.0).astype(jnp.bfloat16)
 
 
-def publish_kernel(width, old, new, mass, rest, live, live_row, bonds, send, pub, own, pad, hold_a, hold_b, s_ref, row_ref):
+def publish_kernel(width, *refs):
+    far, (copies, own, mass_out), near, sems, rest_refs = refs[:8], refs[8:11], refs[11:19], refs[19], refs[20:]
+    moves = [pltpu.make_async_copy(a, b, sems.at[i]) for i, (a, b) in enumerate(zip(far, near))]
+    for move in moves:
+        move.start()
+    for move in moves:
+        move.wait()
+    mass_out[...] = near[2][...]
+    publish_body(width, *near, copies, own, *rest_refs)
+
+
+def publish_body(width, old, new, mass, rest, live, live_row, bonds, send, copies, own, pub, pad, hold_a, hold_b, s_ref, row_ref):
     atoms = SUB * LANES
     sublane = lax.broadcasted_iota(jnp.int32, (SUB, LANES), 0)
     spot = lax.broadcasted_iota(jnp.int32, (SUB, LANES), 1)
@@ -173,6 +184,13 @@
     values = values + [scaling * weight * rest[...], firsts[6], seconds[6]]
     for f, value in enumerate(values):
         pub[f * SUB : (f + 1) * SUB, :] = value
+    block = pub[...]
+
+    def copy(i, carry):
+        copies[i] = block
+        return carry
+
+    lax.fori_loop(0, copies.shape[0], copy, 0)
 
 
 def place(dart):
@@ -486,17 +504,21 @@
     f32, i32 = jnp.float32, jnp.int32
     shape = jax.ShapeDtypeStruct
 
-    pub, own = pl.pallas_call(
+    inputs = (old_pos, new_pos, mass, rest, alive, live.reshape(1, atoms), bond_pairs, send_index)
+    block = (FIELDS * SUB + 24, LANES)
+    pub, own, mass = pl.pallas_call(
         functools.partial(publish_kernel, width),
-        out_shape=[shape((FIELDS * SUB + 24, LANES), f32), shape((3 * SUB, LANES), i32)],
-        in_specs=[VMEM] * 8,
-        out_specs=[VMEM] * 2,
-        scratch_shapes=[pltpu.VMEM(tile, i32)] * 3 + [pltpu.VMEM(tile, f32), pltpu.VMEM((2, atoms), i32)],
+        out_shape=[shape((ny * nz,) + block, f32), shape((3 * SUB, LANES), i32), shape(tile, f32)],
+        in_specs=[pl.BlockSpec(memory_space=pltpu.MemorySpace.HBM)] * len(inputs),
+        out_specs=[VMEM] * 3,
+        scratch_shapes=[pltpu.VMEM(v.shape, v.dtype) for v in inputs]
+        + [pltpu.SemaphoreType.DMA((len(inputs),)), pltpu.VMEM(block, f32)]
+        + [pltpu.VMEM(tile, i32)] * 3
+        + [pltpu.VMEM(tile, f32), pltpu.VMEM((2, atoms), i32)],
         name="publish",
-    )(old_pos, new_pos, mass, rest, alive, live.reshape(1, atoms), bond_pairs, send_index)
-
-    plane = ny * nz
-    gathered = lax.all_to_all(jnp.broadcast_to(pub, (plane,) + pub.shape), ("gy", "gz"), 0, 0)
+    )(*inputs)
+
+    gathered = lax.all_to_all(pub, ("gy", "gz"), 0, 0)
     parts = [gathered]
     for d in range(1, nx):
         parts.append(lax.ppermute(gathered, "gx", [(i, (i - d) % nx) for i in range(nx)]))
@@ -518,6 +540,7 @@
             keep(held, 3), keep(held, 6), keep(held, 2), keep(held), keep(held), keep(held), keep(held), keep(held), keep(held), keep(held),
             pltpu.SMEM((len(near),), i32),
         ],
+        compiler_params=pltpu.CompilerParams(vmem_limit_bytes=24 << 20),
         name="solve",
     )(mass, own, *parts)
     return disp, mult.reshape(atoms)

time: 58 us -> 55.4 us (0.955)
  local copies, waits for them, and re-layouts: 1.84 us -> 0.01 us
  Pallas kernels: 20.8 us -> 19.8 us
    pallas_call x1, Pallas kernels: 18.5 us -> 17.1 us  [per_device(): pl.pallas_call(functools.partial(main_kernel, sizes, width, ranked, count...]
    unnamed x4, local copies, waits for them, and re-layouts: 0.96 us -> 0.01 us
    broadcast_in_dim x1 -> x0, local copies, waits for them, and re-layouts: 0.88 us -> none  [per_device(): jnp.broadcast_to(pub, (plane,) + pub.shape)]
where the time goes in v4:
time: 55.4 us; the launch traced here: 55.1 us
  blocking collectives  32.2 us (58%)
  Pallas kernels  19.8 us (36%)
  waiting for transfers between devices  2.47 us (4%)
  between operations  0.66 us (1%)
    all_to_all x1, blocking collectives, per_device(): gathered = lax.all_to_all(pub, ('gy', 'gz'), 0, 0)  32.2 us
    pallas_call x1, Pallas kernels, per_device(): pl.pallas_call(functools.partial(main_kernel, sizes, width, ranked, count...  17.1 us
    pallas_call x1, Pallas kernels, per_device(): pl.pallas_call(functools.partial(publish_kernel, width), out_shape=[shape...  2.71 us
    ppermute x1, waiting for transfers between devices, per_device(): lax.ppermute(gathered, 'gx', [(i, (i - d) % nx) for i in range(nx)])  2.47 us
  transfers between devices with their start and end apart: 1, of which 1 were waited for; matrix products, arithmetic and copies ran while one was open for 0% of the time, Pallas kernels for 0%

profile of v4, /device:TPU:0, one launch (start us, length us, event | category | flops | bytes accessed | tf_op | source)
XLA Modules:
  0.0 55.1 jit_solution(4169525875386948340)
XLA Ops:
  0.6 2.7 %publish.1 = (f32[16,112,128]{2,1,0:T(8,128)}, s32[24,128]{1,0:T(8,128)}, f32[8,128]{1,0:T(8,128)}) custom-call(f32[3,1024]{1,0:T(4,128)} %refs_0_.1, f32[3,1024]{1,0:T(4,128)} %refs_1_.1, f32[8,128]{1,0:T(8,128)} %bitcast.7, f32[8,128]{1,0:T(8,128)} %bitcast.8, s32[8,128]{1,0:T(8,128)} %bitcast.5, s32[1,1024]{1,0:T(1,128)} %bitcast.6, s32[2,1024]{1,0:T(2,128)} %refs_6_.1, ...), custom_call_target="tpu_custom_call" | custom-call | tf_op jit(solution)/shard_map/publish/pallas_call | solution.py:509
  3.3 0.0 copy-start
  3.4 0.0 copy-start.1
  3.4 32.2 %all_to_all.5.refs_0_ = f32[16,112,128]{2,1,0:T(8,128)S(1)} all-to-all(f32[16,112,128]{2,1,0:T(8,128)} %get-tuple-element.9), channel_id=1, replica_groups=mesh['gx'=2,'gy'=2,'gz'=8] {'gy','gz'}, dimensions={0} | all-to-all | bytes 1835008 | tf_op jit(solution)/shard_map/all_to_all | solution.py:521
  35.5 0.0 collective-permute-start
  35.6 2.5 %collective-permute-done.refs_1_ = f32[16,112,128]{2,1,0:T(8,128)S(1)} collective-permute-done((f32[16,112,128]{2,1,0:T(8,128)S(1)}, f32[16,112,128]{2,1,0:T(8,128)S(1)}, u32[]{:S(2)}, u32[]{:S(2)}) %collective-permute-start) | collective-permute-done | bytes 917536 | tf_op jit(solution)/shard_map/ppermute | solution.py:524
  38.0 0.0 copy-done
  38.0 0.0 copy-done.1
  38.0 17.1 %solve.1 = (f32[3,1024]{1,0:T(4,128)}, f32[8,128]{1,0:T(8,128)}) custom-call(f32[8,128]{1,0:T(8,128)S(1)} %copy-done.1, s32[24,128]{1,0:T(8,128)S(1)} %copy-done, f32[16,112,128]{2,1,0:T(8,128)S(1)} %all_to_all.5.refs_0_, f32[16,112,128]{2,1,0:T(8,128)S(1)} %collective-permute-done.refs_1_), custom_call_target="tpu_custom_call" | custom-call | tf_op jit(solution)/shard_map/solve/pallas_call | solution.py:533
Async XLA Ops:
  3.3 34.7 %copy-start = (s32[24,128]{1,0:T(8,128)S(1)}, s32[24,128]{1,0:T(8,128)}, u32[]{:S(2)}) copy-start(s32[24,128]{1,0:T(8,128)} %get-tuple-element.8.own) | copy-start | bytes 36868
  3.4 34.7 %copy-start.1 = (f32[8,128]{1,0:T(8,128)S(1)}, f32[8,128]{1,0:T(8,128)}, u32[]{:S(2)}) copy-start(f32[8,128]{1,0:T(8,128)} %get-tuple-element.7.mass) | copy-start | bytes 12292
  35.5 2.5 %collective-permute-start = (f32[16,112,128]{2,1,0:T(8,128)S(1)}, f32[16,112,128]{2,1,0:T(8,128)S(1)}, u32[]{:S(2)}, u32[]{:S(2)}) collective-permute-start(f32[16,112,128]{2,1,0:T(8,128)S(1)} %all_to_all.5.refs_0_), channel_id=1, source_target_pairs={{0,16},{16,0},{1,17},{17,1},{2,18},{18,2},{3,19},{19,3},{4,20},{20... | collective-permute-start | bytes 2752520 | tf_op jit(solution)/shard_map/ppermute | solution.py:524

commit v5 on v4

--- a/solution.py
+++ b/solution.py
@@ -14,8 +14,8 @@
 LANES = 128
 HALF = LANES // 2
 SUB = 8
-CHUNK = 16
-LOAD = 4
+CHUNK = 32
+LOAD = 8
 FIELDS = 11
 REACH = 2 * (ORDER + 1)
 VMEM = pl.BlockSpec(memory_space=pltpu.VMEM)
@@ -324,7 +324,8 @@
     def table_of(i, own, ghost):
         rows = {r: functools.partial(own, i, r) for r in range(SUB)}
         for a in range(3):
-            down, up = near[6 * i + 2 * a], near[6 * i + 2 * a + 1]
+            table = near_list if isinstance(i, int) else near
+            down, up = table[6 * i + 2 * a], table[6 * i + 2 * a + 1]
 
             def into(a=a, down=down, up=up):
                 return jnp.where(lower, wide(ghost(up, 4 + a)), wide(ghost(down, 4 + a)))

time: 55.4 us -> 54 us (0.975)
  Pallas kernels: 19.8 us -> 18.4 us
    pallas_call x1, Pallas kernels: 17.1 us -> 15.7 us  [per_device(): pl.pallas_call(functools.partial(main_kernel, sizes, width, ranked, count...]
where the time goes in v5:
time: 54 us; the launch traced here: 53.7 us
  blocking collectives  32.2 us (60%)
  Pallas kernels  18.4 us (34%)
  waiting for transfers between devices  2.47 us (5%)
  between operations  0.66 us (1%)
    all_to_all x1, blocking collectives, per_device(): gathered = lax.all_to_all(pub, ('gy', 'gz'), 0, 0)  32.2 us
    pallas_call x1, Pallas kernels, per_device(): pl.pallas_call(functools.partial(main_kernel, sizes, width, ranked, count...  15.7 us
    pallas_call x1, Pallas kernels, per_device(): pl.pallas_call(functools.partial(publish_kernel, width), out_shape=[shape...  2.71 us
    ppermute x1, waiting for transfers between devices, per_device(): lax.ppermute(gathered, 'gx', [(i, (i - d) % nx) for i in range(nx)])  2.47 us
  transfers between devices with their start and end apart: 1, of which 1 were waited for; matrix products, arithmetic and copies ran while one was open for 0% of the time, Pallas kernels for 0%

profile of v5, /device:TPU:0, one launch (start us, length us, event | category | flops | bytes accessed | tf_op | source)
XLA Modules:
  0.0 53.7 jit_solution(7752041198970442836)
XLA Ops:
  0.6 2.7 %publish.1 = (f32[16,112,128]{2,1,0:T(8,128)}, s32[24,128]{1,0:T(8,128)}, f32[8,128]{1,0:T(8,128)}) custom-call(f32[3,1024]{1,0:T(4,128)} %refs_0_.1, f32[3,1024]{1,0:T(4,128)} %refs_1_.1, f32[8,128]{1,0:T(8,128)} %bitcast.7, f32[8,128]{1,0:T(8,128)} %bitcast.8, s32[8,128]{1,0:T(8,128)} %bitcast.5, s32[1,1024]{1,0:T(1,128)} %bitcast.6, s32[2,1024]{1,0:T(2,128)} %refs_6_.1, ...), custom_call_target="tpu_custom_call" | custom-call | tf_op jit(solution)/shard_map/publish/pallas_call | solution.py:510
  3.3 0.0 copy-start
  3.4 0.0 copy-start.1
  3.4 32.2 %all_to_all.5.refs_0_ = f32[16,112,128]{2,1,0:T(8,128)S(1)} all-to-all(f32[16,112,128]{2,1,0:T(8,128)} %get-tuple-element.9), channel_id=1, replica_groups=mesh['gx'=2,'gy'=2,'gz'=8] {'gy','gz'}, dimensions={0} | all-to-all | bytes 1835008 | tf_op jit(solution)/shard_map/all_to_all | solution.py:522
  35.5 0.0 collective-permute-start
  35.6 2.5 %collective-permute-done.refs_1_ = f32[16,112,128]{2,1,0:T(8,128)S(1)} collective-permute-done((f32[16,112,128]{2,1,0:T(8,128)S(1)}, f32[16,112,128]{2,1,0:T(8,128)S(1)}, u32[]{:S(2)}, u32[]{:S(2)}) %collective-permute-start) | collective-permute-done | bytes 917536 | tf_op jit(solution)/shard_map/ppermute | solution.py:525
  38.0 0.0 copy-done
  38.0 0.0 copy-done.1
  38.0 15.7 %solve.1 = (f32[3,1024]{1,0:T(4,128)}, f32[8,128]{1,0:T(8,128)}) custom-call(f32[8,128]{1,0:T(8,128)S(1)} %copy-done.1, s32[24,128]{1,0:T(8,128)S(1)} %copy-done, f32[16,112,128]{2,1,0:T(8,128)S(1)} %all_to_all.5.refs_0_, f32[16,112,128]{2,1,0:T(8,128)S(1)} %collective-permute-done.refs_1_), custom_call_target="tpu_custom_call" | custom-call | tf_op jit(solution)/shard_map/solve/pallas_call | solution.py:534
Async XLA Ops:
  3.3 34.7 %copy-start = (s32[24,128]{1,0:T(8,128)S(1)}, s32[24,128]{1,0:T(8,128)}, u32[]{:S(2)}) copy-start(s32[24,128]{1,0:T(8,128)} %get-tuple-element.8.own) | copy-start | bytes 36868
  3.4 34.7 %copy-start.1 = (f32[8,128]{1,0:T(8,128)S(1)}, f32[8,128]{1,0:T(8,128)}, u32[]{:S(2)}) copy-start(f32[8,128]{1,0:T(8,128)} %get-tuple-element.7.mass) | copy-start | bytes 12292
  35.5 2.5 %collective-permute-start = (f32[16,112,128]{2,1,0:T(8,128)S(1)}, f32[16,112,128]{2,1,0:T(8,128)S(1)}, u32[]{:S(2)}, u32[]{:S(2)}) collective-permute-start(f32[16,112,128]{2,1,0:T(8,128)S(1)} %all_to_all.5.refs_0_), channel_id=1, source_target_pairs={{0,16},{16,0},{1,17},{17,1},{2,18},{18,2},{3,19},{19,3},{4,20},{20... | collective-permute-start | bytes 2752520 | tf_op jit(solution)/shard_map/ppermute | solution.py:525

commit v6 on v5

--- a/solution.py
+++ b/solution.py
@@ -15,7 +15,7 @@
 HALF = LANES // 2
 SUB = 8
 CHUNK = 32
-LOAD = 8
+LOAD = 16
 FIELDS = 11
 REACH = 2 * (ORDER + 1)
 VMEM = pl.BlockSpec(memory_space=pltpu.VMEM)

time: 54 us -> 54 us (level)
  no operation moved by 1% of the time
where the time goes in v6:
time: 54 us; the launch traced here: 53.7 us
  blocking collectives  32.2 us (60%)
  Pallas kernels  18.4 us (34%)
  waiting for transfers between devices  2.47 us (5%)
  between operations  0.66 us (1%)
    all_to_all x1, blocking collectives, per_device(): gathered = lax.all_to_all(pub, ('gy', 'gz'), 0, 0)  32.2 us
    pallas_call x1, Pallas kernels, per_device(): pl.pallas_call(functools.partial(main_kernel, sizes, width, ranked, count...  15.7 us
    pallas_call x1, Pallas kernels, per_device(): pl.pallas_call(functools.partial(publish_kernel, width), out_shape=[shape...  2.71 us
    ppermute x1, waiting for transfers between devices, per_device(): lax.ppermute(gathered, 'gx', [(i, (i - d) % nx) for i in range(nx)])  2.47 us
  transfers between devices with their start and end apart: 1, of which 1 were waited for; matrix products, arithmetic and copies ran while one was open for 0% of the time, Pallas kernels for 0%

profile of v6, /device:TPU:0, one launch (start us, length us, event | category | flops | bytes accessed | tf_op | source)
XLA Modules:
  0.0 53.7 jit_solution(10817011345958728987)
XLA Ops:
  0.6 2.7 %publish.1 = (f32[16,112,128]{2,1,0:T(8,128)}, s32[24,128]{1,0:T(8,128)}, f32[8,128]{1,0:T(8,128)}) custom-call(f32[3,1024]{1,0:T(4,128)} %refs_0_.1, f32[3,1024]{1,0:T(4,128)} %refs_1_.1, f32[8,128]{1,0:T(8,128)} %bitcast.7, f32[8,128]{1,0:T(8,128)} %bitcast.8, s32[8,128]{1,0:T(8,128)} %bitcast.5, s32[1,1024]{1,0:T(1,128)} %bitcast.6, s32[2,1024]{1,0:T(2,128)} %refs_6_.1, ...), custom_call_target="tpu_custom_call" | custom-call | tf_op jit(solution)/shard_map/publish/pallas_call | solution.py:510
  3.3 0.0 copy-start
  3.4 0.0 copy-start.1
  3.4 32.2 %all_to_all.5.refs_0_ = f32[16,112,128]{2,1,0:T(8,128)S(1)} all-to-all(f32[16,112,128]{2,1,0:T(8,128)} %get-tuple-element.9), channel_id=1, replica_groups=mesh['gx'=2,'gy'=2,'gz'=8] {'gy','gz'}, dimensions={0} | all-to-all | bytes 1835008 | tf_op jit(solution)/shard_map/all_to_all | solution.py:522
  35.5 0.0 collective-permute-start
  35.6 2.5 %collective-permute-done.refs_1_ = f32[16,112,128]{2,1,0:T(8,128)S(1)} collective-permute-done((f32[16,112,128]{2,1,0:T(8,128)S(1)}, f32[16,112,128]{2,1,0:T(8,128)S(1)}, u32[]{:S(2)}, u32[]{:S(2)}) %collective-permute-start) | collective-permute-done | bytes 917536 | tf_op jit(solution)/shard_map/ppermute | solution.py:525
  38.0 0.0 copy-done
  38.0 0.0 copy-done.1
  38.0 15.7 %solve.1 = (f32[3,1024]{1,0:T(4,128)}, f32[8,128]{1,0:T(8,128)}) custom-call(f32[8,128]{1,0:T(8,128)S(1)} %copy-done.1, s32[24,128]{1,0:T(8,128)S(1)} %copy-done, f32[16,112,128]{2,1,0:T(8,128)S(1)} %all_to_all.5.refs_0_, f32[16,112,128]{2,1,0:T(8,128)S(1)} %collective-permute-done.refs_1_), custom_call_target="tpu_custom_call" | custom-call | tf_op jit(solution)/shard_map/solve/pallas_call | solution.py:534
Async XLA Ops:
  3.3 34.7 %copy-start = (s32[24,128]{1,0:T(8,128)S(1)}, s32[24,128]{1,0:T(8,128)}, u32[]{:S(2)}) copy-start(s32[24,128]{1,0:T(8,128)} %get-tuple-element.8.own) | copy-start | bytes 36868
  3.4 34.7 %copy-start.1 = (f32[8,128]{1,0:T(8,128)S(1)}, f32[8,128]{1,0:T(8,128)}, u32[]{:S(2)}) copy-start(f32[8,128]{1,0:T(8,128)} %get-tuple-element.7.mass) | copy-start | bytes 12292
  35.5 2.5 %collective-permute-start = (f32[16,112,128]{2,1,0:T(8,128)S(1)}, f32[16,112,128]{2,1,0:T(8,128)S(1)}, u32[]{:S(2)}, u32[]{:S(2)}) collective-permute-start(f32[16,112,128]{2,1,0:T(8,128)S(1)} %all_to_all.5.refs_0_), channel_id=1, source_target_pairs={{0,16},{16,0},{1,17},{17,1},{2,18},{18,2},{3,19},{19,3},{4,20},{20... | collective-permute-start | bytes 2752520 | tf_op jit(solution)/shard_map/ppermute | solution.py:525
